TPU v7x, 256 devices: a whole 4x4x8 slice. The times are simulated.
256 devices in a mesh: seq: 128 (over x, z_lo, y, core), ch: 2 (over z_hi).
Axes of the slice: x: 4, y: 4, z: 8 (z_hi: 2, z_lo: 4; z = z_hi * 4 + z_lo), core: 2. Of those that a mesh axis runs over, the one named last changes fastest.
Arguments:
- signal: float32 [32768, 256], P('seq', 'ch'), may hold values from -6 to 6
- decay_rate: float32 [256, 64], P('ch'), may hold values from 3.0517578e-05 to 0.05
- frequency: float32 [256, 64], P('ch'), may hold values from 3.0517578e-05 to 0.0078125
- coeff_real: float32 [256, 64], P('ch'), may hold values from -0.5 to 0.5
- coeff_imag: float32 [256, 64], P('ch'), may hold values from -0.5 to 0.5
- skip_weight: float32 [256], P('ch'), may hold values from 0.3 to 3
- norm_gain: float32 [256], P('ch'), may hold values from 0.1 to 1.9
Outputs:
- normed: float32 [32768, 256], P('seq', 'ch')
All inputs are finite; a program needn't handle non-finite values.
Results may differ from a plain program's by a relative error of at most 0.00021.
Values sent between devices are 32-bit elements; how exact they have to be, the bound alone decides.
No kernel may reach another device: no remote copies, remote signals or barrier semaphores. Data moves between devices by JAX's collectives and lax.ppermute only.
A program may use at most 64 MiB of HBM per device.

v0:
```python
import jax
import jax.numpy as jnp
from jax import lax
from jax.experimental import pallas as pl
from jax.experimental.pallas import tpu as pltpu
from jax.sharding import PartitionSpec as P

RADIX = 16
PRECISE = lax.Precision.HIGHEST


def wave(decay, freq, steps):
    mag = jnp.exp(decay * (-float(steps)))
    angle = freq * float(steps)
    return mag * jnp.cos(angle), mag * jnp.sin(angle)


def times(ar, ai, br, bi):
    return ar * br - ai * bi, ar * bi + ai * br


def state_kernel(x_hbm, decay_ref, freq_ref, state_ref, x_ref, table_ref, jump_ref, block_ref, arrived):
    copy = pltpu.make_async_copy(x_hbm, x_ref, arrived)
    copy.start()
    rows = x_ref.shape[0]
    decay, freq = decay_ref[...], freq_ref[...]
    modes = decay.shape[0]
    zr, zi = wave(decay, freq, 1)
    jump_ref[0], jump_ref[1] = wave(decay, freq, RADIX)
    block_ref[0], block_ref[1] = wave(decay, freq, rows)
    table_ref[0, 0] = jnp.ones_like(zr)
    table_ref[1, 0] = jnp.zeros_like(zr)
    pr, pi = zr, zi
    for b in range(1, RADIX):
        table_ref[0, b] = pr
        table_ref[1, b] = pi
        pr, pi = times(pr, pi, zr, zi)
    copy.wait()

    def body(a, carry):
        sr, si = times(*carry, jump_ref[0], jump_ref[1])
        for b in range(RADIX):
            row = x_ref[pl.ds(a * RADIX + b, 1), :]
            sr = sr + row * table_ref[0, RADIX - 1 - b]
            si = si + row * table_ref[1, RADIX - 1 - b]
        return sr, si

    zero = jnp.zeros_like(zr)
    sr, si = lax.fori_loop(0, rows // RADIX, body, (zero, zero))
    state_ref[0:modes] = sr
    state_ref[modes : 2 * modes] = si


def block_powers_kernel(decay_ref, freq_ref, out_ref, *, rows, levels):
    wr = wi = None
    for k in range(1, levels):
        if k % 4 in (0, 1) and k < 5:
            wr, wi = wave(decay_ref[...], freq_ref[...], rows << k)
        else:
            wr, wi = wr * wr - wi * wi, 2.0 * wr * wi
        out_ref[k - 1, 0] = wr
        out_ref[k - 1, 1] = wi


def expand(qr, qi, table_ref, jump_ref, partial, rows):
    modes = qr.shape[0]

    def body(a, carry):
        qr, qi = carry
        for b in range(RADIX):
            value = qr * table_ref[0, b] - qi * table_ref[1, b]
            value = value.reshape(modes // 8, 8, value.shape[1]).sum(axis=0)
            partial[pl.ds((a * RADIX + b) * 8, 8), :] = value
        return times(qr, qi, jump_ref[0], jump_ref[1])

    lax.fori_loop(0, rows // RADIX, body, (qr, qi))


def gathered(partial, group):
    total = partial[pl.ds(group * 64, 8, stride=8), :]
    for i in range(1, 8):
        total = total + partial[pl.ds(group * 64 + i, 8, stride=8), :]
    return total


def taps_kernel(decay_ref, real_ref, imag_ref, table_ref, jump_ref, taps_ref, amp_ref, partial):
    rows = taps_ref.shape[0]
    scale = 2.0 * jnp.sqrt(decay_ref[...])
    ar, ai = scale * real_ref[...], scale * imag_ref[...]
    amp_ref[0], amp_ref[1] = times(ar, ai, table_ref[0, 1], table_ref[1, 1])
    expand(ar, ai, table_ref, jump_ref, partial, rows)
    for g in range(rows // 8):
        taps_ref[8 * g : 8 * g + 8, :] = gathered(partial, g)


def local_kernel(x_ref, taps_ref, skip_ref, out_ref, padded, shifted):
    rows, lanes = x_ref.shape
    padded[0:8] = jnp.zeros((8, lanes), jnp.float32)
    padded[8 : 8 + rows] = x_ref[...]
    for r in range(8):
        shifted[r] = padded[8 - r : 8 - r + rows, :]
    groups = rows // 8

    def body(r, acc):
        acc = list(acc)
        for p in range(groups):
            tap = jnp.broadcast_to(taps_ref[pl.ds(8 * p + r, 1), :], (8, lanes))
            for q in range(p, groups):
                acc[q] = acc[q] + tap * shifted[r, pl.ds(8 * (q - p), 8), :]
        return tuple(acc)

    acc = tuple(skip_ref[...] * x_ref[8 * q : 8 * q + 8, :] for q in range(groups))
    acc = lax.fori_loop(0, 8, body, acc)
    for q in range(groups):
        out_ref[8 * q : 8 * q + 8, :] = acc[q]


def row_sums(values):
    ones = jnp.ones((8, values.shape[1]), jnp.float32)
    return lax.dot_general(ones, values, (((1,), (1,)), ((), ())), precision=PRECISE, preferred_element_type=jnp.float32)


def join_kernel(carry_ref, late_ref, power_ref, amp_ref, table_ref, jump_ref, local_ref, out_ref, stats_ref, partial):
    rows = local_ref.shape[0]
    pr, pi = times(late_ref[0], late_ref[1], power_ref[0], power_ref[1])
    pr, pi = carry_ref[0] + pr, carry_ref[1] + pi
    qr, qi = times(amp_ref[0], amp_ref[1], pr, pi)
    expand(qr, qi, table_ref, jump_ref, partial, rows)
    for g in range(rows // 8):
        at = pl.ds(8 * g, 8)
        out_ref[at, :] = local_ref[at, :] + gathered(partial, g)
    summed = out_ref[...]
    stats_ref[0:8] = row_sums(summed)
    stats_ref[8:16] = row_sums(summed * summed)


def norm_kernel(summed_ref, stats_ref, other_ref, gain_ref, out_ref, *, channels):
    stats = stats_ref[...] + other_ref[...]
    mean = stats[0:8] / channels
    var = stats[8:16] / channels - mean * mean
    scale = lax.rsqrt(var + 1e-05).T[:, 0:1]
    mean = mean.T[:, 0:1]
    out_ref[...] = (summed_ref[...] - mean) * scale * gain_ref[...]


def vmem(*shape):
    return pltpu.VMEM(shape, jnp.float32)


def near(x):
    return pltpu.with_memory_space_constraint(x, pltpu.VMEM)


def after(x, *others):
    return lax.optimization_barrier((x, *others))[0]


def on_device(signal, decay_rate, frequency, coeff_real, coeff_imag, skip_weight, norm_gain):
    rows, lanes = signal.shape
    modes = decay_rate.shape[1]
    shards = lax.axis_size("seq")
    levels = shards.bit_length() - 1
    channels = lanes * lax.axis_size("ch")
    own = lax.axis_index("seq")
    decay, freq, real, imag = decay_rate.T, frequency.T, coeff_real.T, coeff_imag.T
    skip, gain = skip_weight[None, :], norm_gain[None, :]
    partial = vmem(8 * rows, lanes)

    state, x, table, jump, block = pl.pallas_call(
        state_kernel,
        in_specs=[pl.BlockSpec(memory_space=pl.ANY), pl.BlockSpec(), pl.BlockSpec()],
        out_shape=(
            vmem(2 * modes, lanes),
            vmem(rows, lanes),
            vmem(2, RADIX, modes, lanes),
            vmem(2, modes, lanes),
            vmem(2, modes, lanes),
        ),
        scratch_shapes=[pltpu.SemaphoreType.DMA],
        name="state",
    )(signal, decay, freq)
    powers = taps = amp = local = None

    total = state.reshape(2, modes, lanes)
    carry = jnp.zeros_like(total)
    power_r, power_i = jnp.ones((modes, lanes), jnp.float32), jnp.zeros((modes, lanes), jnp.float32)
    late = None
    for k in range(levels):
        late = lax.ppermute(total, "seq", [(i, i ^ (1 << k)) for i in range(shards)])
        upper = (own >> k) & 1 == 1
        if k == 0:
            powers = pl.pallas_call(
                lambda *refs: block_powers_kernel(*refs, rows=rows, levels=levels),
                out_shape=vmem(levels - 1, 2, modes, lanes),
                name="block_powers",
            )(after(decay, total), after(freq, total))
            late, powers = lax.optimization_barrier((late, powers))
        if k == 2:
            taps, amp = pl.pallas_call(
                taps_kernel, out_shape=(vmem(rows, lanes), vmem(2, modes, lanes)), scratch_shapes=[partial], name="taps"
            )(after(decay, total), real, imag, near(table), near(jump))
            late, taps = lax.optimization_barrier((late, taps))
        if k == 4:
            local = pl.pallas_call(
                local_kernel,
                out_shape=vmem(rows, lanes),
                scratch_shapes=[vmem(rows + 8, lanes), vmem(8, rows, lanes)],
                name="local",
            )(near(after(x, total)), near(taps), skip)
            late, local = lax.optimization_barrier((late, local))
        if k + 1 == levels:
            late = jnp.where(upper, late, 0.0)
            break
        add_r, add_i = times(power_r, power_i, late[0], late[1])
        carry = carry + jnp.where(upper, jnp.stack([add_r, add_i]), 0.0)
        wr, wi = (block[0], block[1]) if k == 0 else (powers[k - 1, 0], powers[k - 1, 1])
        low, high = jnp.where(upper, late, total), jnp.where(upper, total, late)
        total = jnp.stack(times(low[0], low[1], wr, wi)) + high
        next_r, next_i = times(power_r, power_i, wr, wi)
        power_r = jnp.where(upper, next_r, power_r)
        power_i = jnp.where(upper, next_i, power_i)

    summed, stats = pl.pallas_call(
        join_kernel, out_shape=(vmem(rows, lanes), vmem(16, rows)), scratch_shapes=[partial], name="join"
    )(
        near(carry),
        near(late),
        near(jnp.stack([power_r, power_i])),
        near(amp),
        near(table),
        near(jump),
        near(local),
    )
    other = lax.ppermute(stats, "ch", [(0, 1), (1, 0)])
    return pl.pallas_call(
        lambda *refs: norm_kernel(*refs, channels=channels),
        out_shape=jax.ShapeDtypeStruct((rows, lanes), jnp.float32),
        name="norm",
    )(near(summed), near(stats), near(other), gain)


def solution(mesh):
    placed = (P("seq", "ch"), P("ch", None), P("ch", None), P("ch", None), P("ch", None), P("ch"), P("ch"))
    return jax.shard_map(on_device, mesh=mesh, in_specs=placed, out_specs=P("seq", "ch"), check_vma=False)
```

profile of v0, /device:TPU:10, one launch (start us, length us, event | category | flops | bytes accessed | tf_op | source)
XLA Modules:
  0.0 48.2 jit_solution(13412844769280221080)
XLA Ops:
  0.0 3.0 %state.1 = (f32[128,128]{1,0:T(8,128)S(1)}, f32[256,128]{1,0:T(8,128)S(1)}, f32[2,16,64,128]{3,2,1,0:T(8,128)S(1)}, f32[2,64,128]{2,1,0:T(8,128)S(1)}, f32[2,64,128]{2,1,0:T(8,128)S(1)}) custom-call(f32[256,128]{1,0:T(8,128)} %x_hbm.1, f32[64,128]{1,0:T(8,128)} %bitcast.176, f32[64,128]{1,0:T(8,128)} %bitcast.179), custom_call_target="tpu_custom_call" | custom-call | tf_op jit(solution)/shard_map/state/pallas_call | solution.py:169
  3.0 0.1 collective-permute-start
  3.1 1.1 %block_powers.1 = f32[6,2,64,128]{3,2,1,0:T(8,128)S(1)} custom-call(f32[64,128]{1,0:T(8,128)} %bitcast.177, f32[64,128]{1,0:T(8,128)} %bitcast.180), custom_call_target="tpu_custom_call" | custom-call | tf_op jit(solution)/shard_map/block_powers/pallas_call | solution.py:192
  4.2 0.2 collective-permute-done
  4.4 0.5 %collective-permute-start.1 = (f32[2,64,128]{2,1,0:T(8,128)S(1)}, f32[2,64,128]{2,1,0:T(8,128)S(1)}, u32[]{:S(2)}, u32[]{:S(2)}) collective-permute-start(f32[2,64,128]{2,1,0:T(8,128)S(1)} %maximum_add_fusion), channel_id=1, source_target_pairs={{0,4},{2,6},{4,0},{6,2},{8,12},{10,14},{12,8},{14,10},{16,20},{18,... | collective-permute-start | bytes 196616 | tf_op jit(solution)/shard_map/ppermute | solution.py:189
  4.9 0.1 fusion.8
  5.0 3.8 %collective-permute-done.1 = f32[2,64,128]{2,1,0:T(8,128)S(1)} collective-permute-done((f32[2,64,128]{2,1,0:T(8,128)S(1)}, f32[2,64,128]{2,1,0:T(8,128)S(1)}, u32[]{:S(2)}, u32[]{:S(2)}) %collective-permute-start.1) | collective-permute-done | bytes 65568 | tf_op jit(solution)/shard_map/ppermute | solution.py:189
  8.9 2.4 %collective-permute-start.2 = (f32[2,64,128]{2,1,0:T(8,128)S(1)}, f32[2,64,128]{2,1,0:T(8,128)S(1)}, u32[]{:S(2)}, u32[]{:S(2)}) collective-permute-start(f32[2,64,128]{2,1,0:T(8,128)S(1)} %maximum_add_fusion.1), channel_id=1, source_target_pairs={{0,8},{2,10},{4,12},{6,14},{8,0},{10,2},{12,4},{14,6},{16,24},{18,... | collective-permute-start | bytes 196616 | tf_op jit(solution)/shard_map/ppermute | solution.py:189
  11.2 2.2 %taps.1 = (f32[256,128]{1,0:T(8,128)S(1)}, f32[2,64,128]{2,1,0:T(8,128)S(1)}) custom-call(f32[64,128]{1,0:T(8,128)} %bitcast.178, f32[64,128]{1,0:T(8,128)} %bitcast.181, f32[64,128]{1,0:T(8,128)} %bitcast.182, f32[2,16,64,128]{3,2,1,0:T(8,128)S(1)} %get-tuple-element.31.table_ref, f32[2,64,128]{2,1,0:T(8,128)S(1)} %get-tuple-element.32.jump_ref), custom_call_target="tpu_custom_call" | custom-call | tf_op jit(solution)/shard_map/taps/pallas_call | solution.py:199
  13.5 1.3 %collective-permute-done.2 = f32[2,64,128]{2,1,0:T(8,128)S(1)} collective-permute-done((f32[2,64,128]{2,1,0:T(8,128)S(1)}, f32[2,64,128]{2,1,0:T(8,128)S(1)}, u32[]{:S(2)}, u32[]{:S(2)}) %collective-permute-start.2) | collective-permute-done | bytes 65568 | tf_op jit(solution)/shard_map/ppermute | solution.py:189
  14.8 2.0 %collective-permute-start.3 = (f32[2,64,128]{2,1,0:T(8,128)S(1)}, f32[2,64,128]{2,1,0:T(8,128)S(1)}, u32[]{:S(2)}, u32[]{:S(2)}) collective-permute-start(f32[2,64,128]{2,1,0:T(8,128)S(1)} %maximum_add_fusion.2), channel_id=1, source_target_pairs={{0,16},{2,18},{4,20},{6,22},{8,24},{10,26},{12,28},{14,30},{16,0},... | collective-permute-start | bytes 196616 | tf_op jit(solution)/shard_map/ppermute | solution.py:189
  16.8 2.3 %collective-permute-done.3 = f32[2,64,128]{2,1,0:T(8,128)S(1)} collective-permute-done((f32[2,64,128]{2,1,0:T(8,128)S(1)}, f32[2,64,128]{2,1,0:T(8,128)S(1)}, u32[]{:S(2)}, u32[]{:S(2)}) %collective-permute-start.3) | collective-permute-done | bytes 65568 | tf_op jit(solution)/shard_map/ppermute | solution.py:189
  19.2 3.4 %collective-permute-start.4 = (f32[2,64,128]{2,1,0:T(8,128)S(1)}, f32[2,64,128]{2,1,0:T(8,128)S(1)}, u32[]{:S(2)}, u32[]{:S(2)}) collective-permute-start(f32[2,64,128]{2,1,0:T(8,128)S(1)} %maximum_add_fusion.3), channel_id=1, source_target_pairs={{0,32},{2,34},{4,36},{6,38},{8,40},{10,42},{12,44},{14,46},{16,48}... | collective-permute-start | bytes 196616 | tf_op jit(solution)/shard_map/ppermute | solution.py:189
  22.5 1.9 %local.1.local_ref = f32[256,128]{1,0:T(8,128)S(1)} custom-call(f32[256,128]{1,0:T(8,128)S(1)} %get-tuple-element.36.x_ref, f32[256,128]{1,0:T(8,128)S(1)} %get-tuple-element.37.taps_ref, f32[1,128]{1,0:T(1,128)} %bitcast.183), custom_call_target="tpu_custom_call" | custom-call | tf_op jit(solution)/shard_map/local/pallas_call | solution.py:204
  24.5 0.3 collective-permute-done.4
  24.8 0.7 %collective-permute-start.5 = (f32[2,64,128]{2,1,0:T(8,128)S(1)}, f32[2,64,128]{2,1,0:T(8,128)S(1)}, u32[]{:S(2)}, u32[]{:S(2)}) collective-permute-start(f32[2,64,128]{2,1,0:T(8,128)S(1)} %maximum_add_fusion.4), channel_id=1, source_target_pairs={{0,64},{2,66},{4,68},{6,70},{8,72},{10,74},{12,76},{14,78},{16,80}... | collective-permute-start | bytes 196616 | tf_op jit(solution)/shard_map/ppermute | solution.py:189
  25.5 3.7 %collective-permute-done.5 = f32[2,64,128]{2,1,0:T(8,128)S(1)} collective-permute-done((f32[2,64,128]{2,1,0:T(8,128)S(1)}, f32[2,64,128]{2,1,0:T(8,128)S(1)}, u32[]{:S(2)}, u32[]{:S(2)}) %collective-permute-start.5) | collective-permute-done | bytes 65568 | tf_op jit(solution)/shard_map/ppermute | solution.py:189
  29.3 2.2 %collective-permute-start.6 = (f32[2,64,128]{2,1,0:T(8,128)S(1)}, f32[2,64,128]{2,1,0:T(8,128)S(1)}, u32[]{:S(2)}, u32[]{:S(2)}) collective-permute-start(f32[2,64,128]{2,1,0:T(8,128)S(1)} %maximum_add_fusion.5), channel_id=1, source_target_pairs={{0,128},{2,130},{4,132},{6,134},{8,136},{10,138},{12,140},{14,142}... | collective-permute-start | bytes 196616 | tf_op jit(solution)/shard_map/ppermute | solution.py:189
  31.5 3.6 %collective-permute-done.6 = f32[2,64,128]{2,1,0:T(8,128)S(1)} collective-permute-done((f32[2,64,128]{2,1,0:T(8,128)S(1)}, f32[2,64,128]{2,1,0:T(8,128)S(1)}, u32[]{:S(2)}, u32[]{:S(2)}) %collective-permute-start.6) | collective-permute-done | bytes 65568 | tf_op jit(solution)/shard_map/ppermute | solution.py:189
  35.1 1.7 %join.1 = (f32[256,128]{1,0:T(8,128)S(1)}, f32[16,256]{1,0:T(8,128)S(1)}) custom-call(f32[2,64,128]{2,1,0:T(8,128)S(1)} %fusion.4.carry_ref, f32[2,64,128]{2,1,0:T(8,128)S(1)} %broadcast_select_fusion.late_ref, f32[2,64,128]{2,1,0:T(8,128)S(1)} %pad_maximum_fusion.power_ref, f32[2,64,128]{2,1,0:T(8,128)S(1)} %get-tuple-element.39.amp_ref, ...), custom_call_target="tpu_custom_call" | custom-call | tf_op jit(solution)/shard_map/join/pallas_call | solution.py:223
  36.8 8.1 %collective-permute-start.7 = (f32[16,256]{1,0:T(8,128)S(1)}, f32[16,256]{1,0:T(8,128)S(1)}, u32[]{:S(2)}, u32[]{:S(2)}) collective-permute-start(f32[16,256]{1,0:T(8,128)S(1)} %get-tuple-element.42.refs_1_), channel_id=1, source_target_pairs={{0,1},{1,0},{2,3},{3,2},{4,5},{5,4},{6,7},{7,6},{8,9},{9,8},{10,11... | collective-permute-start | bytes 49160 | tf_op jit(solution)/shard_map/ppermute | solution.py:234
  44.9 1.7 %collective-permute-done.7.refs_2_ = f32[16,256]{1,0:T(8,128)S(1)} collective-permute-done((f32[16,256]{1,0:T(8,128)S(1)}, f32[16,256]{1,0:T(8,128)S(1)}, u32[]{:S(2)}, u32[]{:S(2)}) %collective-permute-start.7) | collective-permute-done | bytes 16416 | tf_op jit(solution)/shard_map/ppermute | solution.py:234
  46.7 1.6 %norm.1 = f32[256,128]{1,0:T(8,128)} custom-call(f32[256,128]{1,0:T(8,128)S(1)} %get-tuple-element.41.refs_0_, f32[16,256]{1,0:T(8,128)S(1)} %get-tuple-element.42.refs_1_, f32[16,256]{1,0:T(8,128)S(1)} %collective-permute-done.7.refs_2_, f32[1,128]{1,0:T(1,128)} %bitcast.184), custom_call_target="tpu_custom_call" | custom-call | tf_op jit(solution)/shard_map/norm/pallas_call | solution.py:235
  (26 shorter events, 0.3 us)
Async XLA Ops:
  3.0 1.3 %collective-permute-start = (f32[2,64,128]{2,1,0:T(8,128)S(1)}, f32[2,64,128]{2,1,0:T(8,128)S(1)}, u32[]{:S(2)}, u32[]{:S(2)}) collective-permute-start(f32[2,64,128]{2,1,0:T(8,128)S(1)} %bitcast.173), channel_id=1, source_target_pairs={{0,2},{2,0},{4,6},{6,4},{8,10},{10,8},{12,14},{14,12},{16,18},{18,... | collective-permute-start | bytes 196616 | tf_op jit(solution)/shard_map/ppermute | solution.py:189
  4.4 4.4 %collective-permute-start.1 = (f32[2,64,128]{2,1,0:T(8,128)S(1)}, f32[2,64,128]{2,1,0:T(8,128)S(1)}, u32[]{:S(2)}, u32[]{:S(2)}) collective-permute-start(f32[2,64,128]{2,1,0:T(8,128)S(1)} %maximum_add_fusion), channel_id=1, source_target_pairs={{0,4},{2,6},{4,0},{6,2},{8,12},{10,14},{12,8},{14,10},{16,20},{18,... | collective-permute-start | bytes 196616 | tf_op jit(solution)/shard_map/ppermute | solution.py:189
  8.9 5.9 %collective-permute-start.2 = (f32[2,64,128]{2,1,0:T(8,128)S(1)}, f32[2,64,128]{2,1,0:T(8,128)S(1)}, u32[]{:S(2)}, u32[]{:S(2)}) collective-permute-start(f32[2,64,128]{2,1,0:T(8,128)S(1)} %maximum_add_fusion.1), channel_id=1, source_target_pairs={{0,8},{2,10},{4,12},{6,14},{8,0},{10,2},{12,4},{14,6},{16,24},{18,... | collective-permute-start | bytes 196616 | tf_op jit(solution)/shard_map/ppermute | solution.py:189
  14.8 4.4 %collective-permute-start.3 = (f32[2,64,128]{2,1,0:T(8,128)S(1)}, f32[2,64,128]{2,1,0:T(8,128)S(1)}, u32[]{:S(2)}, u32[]{:S(2)}) collective-permute-start(f32[2,64,128]{2,1,0:T(8,128)S(1)} %maximum_add_fusion.2), channel_id=1, source_target_pairs={{0,16},{2,18},{4,20},{6,22},{8,24},{10,26},{12,28},{14,30},{16,0},... | collective-permute-start | bytes 196616 | tf_op jit(solution)/shard_map/ppermute | solution.py:189
  19.2 5.6 %collective-permute-start.4 = (f32[2,64,128]{2,1,0:T(8,128)S(1)}, f32[2,64,128]{2,1,0:T(8,128)S(1)}, u32[]{:S(2)}, u32[]{:S(2)}) collective-permute-start(f32[2,64,128]{2,1,0:T(8,128)S(1)} %maximum_add_fusion.3), channel_id=1, source_target_pairs={{0,32},{2,34},{4,36},{6,38},{8,40},{10,42},{12,44},{14,46},{16,48}... | collective-permute-start | bytes 196616 | tf_op jit(solution)/shard_map/ppermute | solution.py:189
  24.8 4.4 %collective-permute-start.5 = (f32[2,64,128]{2,1,0:T(8,128)S(1)}, f32[2,64,128]{2,1,0:T(8,128)S(1)}, u32[]{:S(2)}, u32[]{:S(2)}) collective-permute-start(f32[2,64,128]{2,1,0:T(8,128)S(1)} %maximum_add_fusion.4), channel_id=1, source_target_pairs={{0,64},{2,66},{4,68},{6,70},{8,72},{10,74},{12,76},{14,78},{16,80}... | collective-permute-start | bytes 196616 | tf_op jit(solution)/shard_map/ppermute | solution.py:189
  29.3 5.9 %collective-permute-start.6 = (f32[2,64,128]{2,1,0:T(8,128)S(1)}, f32[2,64,128]{2,1,0:T(8,128)S(1)}, u32[]{:S(2)}, u32[]{:S(2)}) collective-permute-start(f32[2,64,128]{2,1,0:T(8,128)S(1)} %maximum_add_fusion.5), channel_id=1, source_target_pairs={{0,128},{2,130},{4,132},{6,134},{8,136},{10,138},{12,140},{14,142}... | collective-permute-start | bytes 196616 | tf_op jit(solution)/shard_map/ppermute | solution.py:189
  36.8 9.8 %collective-permute-start.7 = (f32[16,256]{1,0:T(8,128)S(1)}, f32[16,256]{1,0:T(8,128)S(1)}, u32[]{:S(2)}, u32[]{:S(2)}) collective-permute-start(f32[16,256]{1,0:T(8,128)S(1)} %get-tuple-element.42.refs_1_), channel_id=1, source_target_pairs={{0,1},{1,0},{2,3},{3,2},{4,5},{5,4},{6,7},{7,6},{8,9},{9,8},{10,11... | collective-permute-start | bytes 49160 | tf_op jit(solution)/shard_map/ppermute | solution.py:234
where the time goes:
time: 48.6 us; the launch traced here: 48.2 us
  starting transfers between devices  19.4 us (40%)
  waiting for transfers between devices  16.9 us (35%)
  Pallas kernels  11.5 us (24%)
    ppermute x7, waiting for transfers between devices, on_device(): late = lax.ppermute(total, 'seq', [(i, i ^ 1 << k) for i in range(shards)])  15.1 us
    ppermute x7, starting transfers between devices, on_device(): late = lax.ppermute(total, 'seq', [(i, i ^ 1 << k) for i in range(shards)])  11.3 us
    ppermute x1, starting transfers between devices, on_device(): other = lax.ppermute(stats, 'ch', [(0, 1), (1, 0)])  8.1 us
    pallas_call x1, Pallas kernels, on_device(): pl.pallas_call(state_kernel, in_specs=[pl.BlockSpec(memory_space=pl.ANY),...  2.98 us
    pallas_call x1, Pallas kernels, on_device(): pl.pallas_call(taps_kernel, out_shape=(vmem(rows, lanes), vmem(2, modes,...  2.2 us
    pallas_call x1, Pallas kernels, on_device(): pl.pallas_call(local_kernel, out_shape=vmem(rows, lanes), scratch_shapes=...  1.93 us
    ppermute x1, waiting for transfers between devices, on_device(): other = lax.ppermute(stats, 'ch', [(0, 1), (1, 0)])  1.72 us
    pallas_call x1, Pallas kernels, on_device(): pl.pallas_call(join_kernel, out_shape=(vmem(rows, lanes), vmem(16, rows))...  1.71 us
  transfers between devices with their start and end apart: 8, of which 8 were waited for; matrix products, arithmetic and copies ran while one was open for 0% of the time, Pallas kernels for 11%

commit v1 on v0

v1 whole, which is shorter than its diff:
```python
import jax
import jax.numpy as jnp
from jax import lax
from jax.experimental import pallas as pl
from jax.experimental.pallas import tpu as pltpu
from jax.sharding import PartitionSpec as P

RADIX = 16
PRECISE = lax.Precision.HIGHEST


def wave(decay, freq, steps):
    mag = jnp.exp(decay * (-float(steps)))
    angle = freq * float(steps)
    return mag * jnp.cos(angle), mag * jnp.sin(angle)


def times(ar, ai, br, bi):
    return ar * br - ai * bi, ar * bi + ai * br


def fill_powers(table_ref, zr, zi):
    table_ref[0, 0] = jnp.ones_like(zr)
    table_ref[1, 0] = jnp.zeros_like(zr)
    pr, pi = zr, zi
    for b in range(1, RADIX):
        table_ref[0, b] = pr
        table_ref[1, b] = pi
        if b + 1 < RADIX:
            pr, pi = times(pr, pi, zr, zi)


def reduced(x_ref, table_ref, jump_ref):
    def body(a, carry):
        sr, si = times(*carry, jump_ref[0], jump_ref[1])
        for b in range(RADIX):
            row = x_ref[pl.ds(a * RADIX + b, 1), :]
            sr = sr + row * table_ref[0, RADIX - 1 - b]
            si = si + row * table_ref[1, RADIX - 1 - b]
        return sr, si

    zero = jnp.zeros(jump_ref.shape[1:], jnp.float32)
    return lax.fori_loop(0, x_ref.shape[0] // RADIX, body, (zero, zero))


def half_of_modes(modes, other=0):
    half = modes // 2
    return pl.ds(pl.multiple_of((lax.axis_index("seq") % 2 + other) % 2 * half, half), half)


def own_state_kernel(x_hbm, decay_ref, freq_ref, state_ref, x_ref, table_ref, jump_ref, block_ref, arrived):
    copy = pltpu.make_async_copy(x_hbm, x_ref, arrived)
    copy.start()
    mine = half_of_modes(decay_ref.shape[0])
    decay, freq = decay_ref[mine, :], freq_ref[mine, :]
    zr, zi = wave(decay, freq, 1)
    jump_ref[0], jump_ref[1] = wave(decay, freq, RADIX)
    block_ref[0], block_ref[1] = wave(decay, freq, x_ref.shape[0])
    fill_powers(table_ref, zr, zi)
    copy.wait()
    state_ref[0], state_ref[1] = reduced(x_ref, table_ref, jump_ref)


def chip_state_kernel(x_ref, table_ref, jump_ref, block_ref, state_ref, total_ref, first_ref):
    other = reduced(x_ref, table_ref, jump_ref)
    odd = lax.axis_index("seq") % 2 == 1
    firsts = [jnp.where(odd, other[i], state_ref[i]) for i in (0, 1)]
    seconds = [jnp.where(odd, state_ref[i], other[i]) for i in (0, 1)]
    moved = times(*firsts, block_ref[0], block_ref[1])
    for i in (0, 1):
        first_ref[i] = firsts[i]
        total_ref[i] = moved[i] + seconds[i]


def chip_powers_kernel(block_ref, decay_ref, freq_ref, out_ref, *, rows):
    mine = half_of_modes(decay_ref.shape[0])
    wr, wi = block_ref[0], block_ref[1]
    for k in range(out_ref.shape[0]):
        if k == 3:
            wr, wi = wave(decay_ref[mine, :], freq_ref[mine, :], 2 * rows << k)
        else:
            wr, wi = wr * wr - wi * wi, 2.0 * wr * wi
        out_ref[k, 0] = wr
        out_ref[k, 1] = wi


def expand(qr, qi, table_ref, jump_ref, at, partial, rows):
    modes = qr.shape[0]

    def body(a, carry):
        qr, qi = carry
        for b in range(RADIX):
            value = qr * table_ref[0, b, at, :] - qi * table_ref[1, b, at, :]
            value = value.reshape(modes // 8, 8, value.shape[1]).sum(axis=0)
            partial[pl.ds((a * RADIX + b) * 8, 8), :] = value
        return times(qr, qi, jump_ref[0, at, :], jump_ref[1, at, :])

    lax.fori_loop(0, rows // RADIX, body, (qr, qi))


def gathered(partial, group):
    total = partial[pl.ds(group * 64, 8, stride=8), :]
    for i in range(1, 8):
        total = total + partial[pl.ds(group * 64 + i, 8, stride=8), :]
    return total


def taps_kernel(decay_ref, freq_ref, real_ref, imag_ref, gain_in, taps_ref, amp_ref, table_ref, jump_ref, gain_ref, partial):
    rows, modes = taps_ref.shape[0], decay_ref.shape[0]
    gain_ref[...] = gain_in[...]
    scale = 2.0 * jnp.sqrt(decay_ref[...])
    ar, ai = scale * real_ref[...], scale * imag_ref[...]
    zr, zi = wave(decay_ref[...], freq_ref[...], 1)
    jump_ref[0], jump_ref[1] = wave(decay_ref[...], freq_ref[...], RADIX)
    amp_ref[0], amp_ref[1] = times(ar, ai, zr, zi)
    fill_powers(table_ref, zr, zi)
    expand(ar, ai, table_ref, jump_ref, pl.ds(0, modes), partial, rows)
    for g in range(rows // 8):
        taps_ref[8 * g : 8 * g + 8, :] = gathered(partial, g)


def local_kernel(x_ref, taps_ref, skip_ref, out_ref, padded, shifted):
    rows, lanes = x_ref.shape
    padded[0:8] = jnp.zeros((8, lanes), jnp.float32)
    padded[8 : 8 + rows] = x_ref[...]
    for r in range(8):
        shifted[r] = padded[8 - r : 8 - r + rows, :]
    groups = rows // 8

    def body(r, acc):
        acc = list(acc)
        for p in range(groups):
            tap = jnp.broadcast_to(taps_ref[pl.ds(8 * p + r, 1), :], (8, lanes))
            for q in range(p, groups):
                acc[q] = acc[q] + tap * shifted[r, pl.ds(8 * (q - p), 8), :]
        return tuple(acc)

    acc = tuple(skip_ref[...] * x_ref[8 * q : 8 * q + 8, :] for q in range(groups))
    acc = lax.fori_loop(0, 8, body, acc)
    for q in range(groups):
        out_ref[8 * q : 8 * q + 8, :] = acc[q]


def row_sums(values):
    ones = jnp.ones((8, values.shape[1]), jnp.float32)
    return lax.dot_general(ones, values, (((1,), (1,)), ((), ())), precision=PRECISE, preferred_element_type=jnp.float32)


def add_carried(carry_ref, amp_ref, table_ref, jump_ref, base_ref, out_ref, partial, other):
    rows = base_ref.shape[0]
    at = half_of_modes(amp_ref.shape[1], other)
    qr, qi = times(amp_ref[0, at, :], amp_ref[1, at, :], carry_ref[0], carry_ref[1])
    expand(qr, qi, table_ref, jump_ref, at, partial, rows)
    for g in range(rows // 8):
        out_ref[8 * g : 8 * g + 8, :] = base_ref[8 * g : 8 * g + 8, :] + gathered(partial, g)


def own_half_kernel(carry_ref, amp_ref, table_ref, jump_ref, base_ref, out_ref, partial):
    add_carried(carry_ref, amp_ref, table_ref, jump_ref, base_ref, out_ref, partial, 0)


def other_half_kernel(carry_ref, amp_ref, table_ref, jump_ref, base_ref, out_ref, stats_ref, partial):
    add_carried(carry_ref, amp_ref, table_ref, jump_ref, base_ref, out_ref, partial, 1)
    summed = out_ref[...]
    stats_ref[0:1] = row_sums(summed)[0:1]
    stats_ref[1:2] = row_sums(summed * summed)[0:1]


def norm_kernel(summed_ref, stats_ref, other_ref, gain_ref, out_ref, *, channels):
    stats = stats_ref[...] + other_ref[...]
    mean = stats[0:1] / channels
    var = stats[1:2] / channels - mean * mean
    scale = lax.rsqrt(var + 1e-05)
    width = stats.shape[1]
    column = jnp.concatenate([jnp.broadcast_to(mean, (8, width)), jnp.broadcast_to(scale, (8, width))]).T
    out_ref[...] = (summed_ref[...] - column[:, 0:1]) * column[:, 8:9] * gain_ref[...]


def vmem(*shape):
    return pltpu.VMEM(shape, jnp.float32)


def near(x):
    return pltpu.with_memory_space_constraint(x, pltpu.VMEM)


def after(x, *others):
    return lax.optimization_barrier((x, *others))[0]


def on_device(signal, decay_rate, frequency, coeff_real, coeff_imag, skip_weight, norm_gain):
    rows, lanes = signal.shape
    modes = decay_rate.shape[1]
    half = modes // 2
    shards = lax.axis_size("seq")
    channels = lanes * lax.axis_size("ch")
    own = lax.axis_index("seq")
    decay, freq, real, imag = decay_rate.T, frequency.T, coeff_real.T, coeff_imag.T
    skip, gain = skip_weight[None, :], norm_gain[None, :]
    partial = vmem(8 * rows, lanes)
    core_pairs = [(i, i ^ 1) for i in range(shards)]

    other_x = lax.ppermute(signal, "seq", core_pairs)
    state, x, own_table, own_jump, block = pl.pallas_call(
        own_state_kernel,
        in_specs=[pl.BlockSpec(memory_space=pl.ANY), pl.BlockSpec(), pl.BlockSpec()],
        out_shape=(
            vmem(2, half, lanes),
            vmem(rows, lanes),
            vmem(2, RADIX, half, lanes),
            vmem(2, half, lanes),
            vmem(2, half, lanes),
        ),
        scratch_shapes=[pltpu.SemaphoreType.DMA],
        name="own_state",
    )(signal, decay, freq)
    other_x, state = lax.optimization_barrier((other_x, state))
    total, first = pl.pallas_call(
        chip_state_kernel, out_shape=(vmem(2, half, lanes), vmem(2, half, lanes)), name="chip_state"
    )(near(other_x), near(own_table), near(own_jump), near(block), near(state))

    partners = (2, 6, 8, 16, 32, 96)
    carry = jnp.zeros_like(total)
    power_r, power_i = jnp.ones((half, lanes), jnp.float32), jnp.zeros((half, lanes), jnp.float32)
    powers = taps = local = late = None
    for k, partner in enumerate(partners):
        late = lax.ppermute(total, "seq", [(i, i ^ partner) for i in range(shards)])
        upper = (own >> (k + 1)) & 1 == 1
        if k == 0:
            powers = pl.pallas_call(
                lambda *refs: chip_powers_kernel(*refs, rows=rows),
                out_shape=vmem(len(partners), 2, half, lanes),
                name="chip_powers",
            )(near(after(block, total)), decay, freq)
            late, powers = lax.optimization_barrier((late, powers))
        if k == 1:
            taps, amp, table, jump, gain = pl.pallas_call(
                taps_kernel,
                out_shape=(
                    vmem(rows, lanes),
                    vmem(2, modes, lanes),
                    vmem(2, RADIX, modes, lanes),
                    vmem(2, modes, lanes),
                    vmem(1, lanes),
                ),
                scratch_shapes=[partial],
                name="taps",
            )(after(decay, total), freq, real, imag, gain)
            late, taps = lax.optimization_barrier((late, taps))
        if k == 3:
            local = pl.pallas_call(
                local_kernel,
                out_shape=vmem(rows, lanes),
                scratch_shapes=[vmem(rows + 8, lanes), vmem(8, rows, lanes)],
                name="local",
            )(near(after(x, total)), near(taps), skip)
            late, local = lax.optimization_barrier((late, local))
        add_r, add_i = times(power_r, power_i, late[0], late[1])
        carry = carry + jnp.where(upper, jnp.stack([add_r, add_i]), 0.0)
        if k + 1 == len(partners):
            break
        wr, wi = powers[k, 0], powers[k, 1]
        low, high = jnp.where(upper, late, total), jnp.where(upper, total, late)
        total = jnp.stack(times(low[0], low[1], wr, wi)) + high
        next_r, next_i = times(power_r, power_i, wr, wi)
        power_r = jnp.where(upper, next_r, power_r)
        power_i = jnp.where(upper, next_i, power_i)

    odd = own % 2 == 1
    second = jnp.stack(times(carry[0], carry[1], block[0], block[1])) + first
    own_carry, other_carry = jnp.where(odd, second, carry), jnp.where(odd, carry, second)
    other_carry = lax.ppermute(other_carry, "seq", core_pairs)
    part = pl.pallas_call(own_half_kernel, out_shape=vmem(rows, lanes), scratch_shapes=[partial], name="own_half")(
        near(own_carry), near(amp), near(table), near(jump), near(local)
    )
    other_carry, part = lax.optimization_barrier((other_carry, part))
    summed, stats = pl.pallas_call(
        other_half_kernel,
        out_shape=(vmem(rows, lanes), vmem(2, rows)),
        scratch_shapes=[partial],
        name="other_half",
    )(near(other_carry), near(amp), near(table), near(jump), near(part))
    other = lax.ppermute(stats, "ch", [(0, 1), (1, 0)])
    return pl.pallas_call(
        lambda *refs: norm_kernel(*refs, channels=channels),
        out_shape=jax.ShapeDtypeStruct((rows, lanes), jnp.float32),
        name="norm",
    )(near(summed), near(stats), near(other), near(gain))


def solution(mesh):
    placed = (P("seq", "ch"), P("ch", None), P("ch", None), P("ch", None), P("ch", None), P("ch"), P("ch"))
    return jax.shard_map(on_device, mesh=mesh, in_specs=placed, out_specs=P("seq", "ch"), check_vma=False)
```

time: 48.6 us -> 43.9 us (0.903)
  the two profiles are of different devices: /device:TPU:10 before, /device:TPU:1 now
where the time goes in v1:
time: 43.9 us; the launch traced here: 43.6 us
  starting transfers between devices  23.7 us (54%)
  Pallas kernels  11.2 us (26%)
  waiting for transfers between devices  8.25 us (19%)
    ppermute x6, starting transfers between devices, on_device(): late = lax.ppermute(total, 'seq', [(i, i ^ partner) for i in range(shards)])  9.12 us
    ppermute x6, waiting for transfers between devices, on_device(): late = lax.ppermute(total, 'seq', [(i, i ^ partner) for i in range(shards)])  7.22 us
    ppermute x1, starting transfers between devices, on_device(): other = lax.ppermute(stats, 'ch', [(0, 1), (1, 0)])  5.7 us
    ppermute x1, starting transfers between devices, on_device(): other_carry = lax.ppermute(other_carry, 'seq', core_pairs)  5.67 us
    ppermute x1, starting transfers between devices, on_device(): other_x = lax.ppermute(signal, 'seq', core_pairs)  3.2 us
    pallas_call x1, Pallas kernels, on_device(): pl.pallas_call(taps_kernel, out_shape=(vmem(rows, lanes), vmem(2, modes,...  2.57 us
    pallas_call x1, Pallas kernels, on_device(): pl.pallas_call(own_state_kernel, in_specs=[pl.BlockSpec(memory_space=pl.A...  2.37 us
    pallas_call x1, Pallas kernels, on_device(): pl.pallas_call(local_kernel, out_shape=vmem(rows, lanes), scratch_shapes=...  1.93 us
  transfers between devices with their start and end apart: 9, of which 7 were waited for; matrix products, arithmetic and copies ran while one was open for 0% of the time, Pallas kernels for 20%

profile of v1, /device:TPU:1, one launch (start us, length us, event | category | flops | bytes accessed | tf_op | source)
XLA Modules:
  0.0 43.6 jit_solution(8444003234231150321)
XLA Ops:
  0.0 3.2 %collective-permute-start = (f32[256,128]{1,0:T(8,128)}, f32[256,128]{1,0:T(8,128)S(1)}, u32[]{:S(2)}, u32[]{:S(2)}) collective-permute-start(f32[256,128]{1,0:T(8,128)} %x_hbm.1), channel_id=1, source_target_pairs={{0,2},{2,0},{4,6},{6,4},{8,10},{10,8},{12,14},{14,12},{16,18},{18,... | collective-permute-start | bytes 393224 | tf_op jit(solution)/shard_map/ppermute | solution.py:203
  3.2 2.4 %own_state.1 = (f32[2,32,128]{2,1,0:T(8,128)S(1)}, f32[256,128]{1,0:T(8,128)S(1)}, f32[2,16,32,128]{3,2,1,0:T(8,128)S(1)}, f32[2,32,128]{2,1,0:T(8,128)S(1)}, f32[2,32,128]{2,1,0:T(8,128)S(1)}) custom-call(f32[256,128]{1,0:T(8,128)} %x_hbm.1, f32[64,128]{1,0:T(8,128)} %bitcast.172, f32[64,128]{1,0:T(8,128)} %bitcast.175), custom_call_target="tpu_custom_call" | custom-call | tf_op jit(solution)/shard_map/own_state/pallas_call | solution.py:204
  5.6 0.0 collective-permute-done.x_ref
  5.6 0.7 %chip_state.1 = (f32[2,32,128]{2,1,0:T(8,128)S(1)}, f32[2,32,128]{2,1,0:T(8,128)S(1)}) custom-call(f32[256,128]{1,0:T(8,128)S(1)} %collective-permute-done.x_ref, f32[2,16,32,128]{3,2,1,0:T(8,128)S(1)} %get-tuple-element.34.table_ref, f32[2,32,128]{2,1,0:T(8,128)S(1)} %get-tuple-element.35.jump_ref, f32[2,32,128]{2,1,0:T(8,128)S(1)} %get-tuple-element.39.block_ref.refs_0_, ...), custom_call_target="tpu_custom_call" | custom-call | tf_op jit(solution)/shard_map/chip_state/pallas_call | solution.py:218
  6.3 0.1 collective-permute-start.1
  6.4 0.9 %chip_powers.1 = f32[6,2,32,128]{3,2,1,0:T(8,128)S(1)} custom-call(f32[2,32,128]{2,1,0:T(8,128)S(1)} %get-tuple-element.39.block_ref.refs_0_, f32[64,128]{1,0:T(8,128)} %bitcast.173, f32[64,128]{1,0:T(8,128)} %bitcast.176), custom_call_target="tpu_custom_call" | custom-call | tf_op jit(solution)/shard_map/chip_powers/pallas_call | solution.py:230
  7.3 1.9 %collective-permute-done.1 = f32[2,32,128]{2,1,0:T(8,128)S(1)} collective-permute-done((f32[2,32,128]{2,1,0:T(8,128)S(1)}, f32[2,32,128]{2,1,0:T(8,128)S(1)}, u32[]{:S(2)}, u32[]{:S(2)}) %collective-permute-start.1) | collective-permute-done | bytes 32800 | tf_op jit(solution)/shard_map/ppermute | solution.py:227
  9.2 1.1 %collective-permute-start.2 = (f32[2,32,128]{2,1,0:T(8,128)S(1)}, f32[2,32,128]{2,1,0:T(8,128)S(1)}, u32[]{:S(2)}, u32[]{:S(2)}) collective-permute-start(f32[2,32,128]{2,1,0:T(8,128)S(1)} %maximum_add_fusion), channel_id=1, source_target_pairs={{0,12},{2,14},{4,8},{6,10},{8,4},{10,6},{12,0},{14,2},{16,28},{18,... | collective-permute-start | bytes 98312 | tf_op jit(solution)/shard_map/ppermute | solution.py:227
  10.3 2.6 %taps.1 = (f32[256,128]{1,0:T(8,128)S(1)}, f32[2,64,128]{2,1,0:T(8,128)S(1)}, f32[2,16,64,128]{3,2,1,0:T(8,128)S(1)}, f32[2,64,128]{2,1,0:T(8,128)S(1)}, f32[1,128]{1,0:T(1,128)S(1)}) custom-call(f32[64,128]{1,0:T(8,128)} %bitcast.174, f32[64,128]{1,0:T(8,128)} %bitcast.177, f32[64,128]{1,0:T(8,128)} %bitcast.178, f32[64,128]{1,0:T(8,128)} %bitcast.179, ...), custom_call_target="tpu_custom_call" | custom-call | tf_op jit(solution)/shard_map/taps/pallas_call | solution.py:237
  12.9 0.4 collective-permute-done.2
  13.3 1.4 %collective-permute-start.3 = (f32[2,32,128]{2,1,0:T(8,128)S(1)}, f32[2,32,128]{2,1,0:T(8,128)S(1)}, u32[]{:S(2)}, u32[]{:S(2)}) collective-permute-start(f32[2,32,128]{2,1,0:T(8,128)S(1)} %maximum_add_fusion.1), channel_id=1, source_target_pairs={{0,16},{2,18},{4,20},{6,22},{8,24},{10,26},{12,28},{14,30},{16,0},... | collective-permute-start | bytes 98312 | tf_op jit(solution)/shard_map/ppermute | solution.py:227
  14.7 1.5 %collective-permute-done.3 = f32[2,32,128]{2,1,0:T(8,128)S(1)} collective-permute-done((f32[2,32,128]{2,1,0:T(8,128)S(1)}, f32[2,32,128]{2,1,0:T(8,128)S(1)}, u32[]{:S(2)}, u32[]{:S(2)}) %collective-permute-start.3) | collective-permute-done | bytes 32800 | tf_op jit(solution)/shard_map/ppermute | solution.py:227
  16.2 2.9 %collective-permute-start.4 = (f32[2,32,128]{2,1,0:T(8,128)S(1)}, f32[2,32,128]{2,1,0:T(8,128)S(1)}, u32[]{:S(2)}, u32[]{:S(2)}) collective-permute-start(f32[2,32,128]{2,1,0:T(8,128)S(1)} %maximum_add_fusion.2), channel_id=1, source_target_pairs={{0,32},{2,34},{4,36},{6,38},{8,40},{10,42},{12,44},{14,46},{16,48}... | collective-permute-start | bytes 98312 | tf_op jit(solution)/shard_map/ppermute | solution.py:227
  19.1 1.9 %local.1.base_ref = f32[256,128]{1,0:T(8,128)S(1)} custom-call(f32[256,128]{1,0:T(8,128)S(1)} %get-tuple-element.46.x_ref, f32[256,128]{1,0:T(8,128)S(1)} %get-tuple-element.47.taps_ref, f32[1,128]{1,0:T(1,128)} %bitcast.181), custom_call_target="tpu_custom_call" | custom-call | tf_op jit(solution)/shard_map/local/pallas_call | solution.py:251
  21.0 0.0 collective-permute-done.4
  21.1 1.3 %collective-permute-start.5 = (f32[2,32,128]{2,1,0:T(8,128)S(1)}, f32[2,32,128]{2,1,0:T(8,128)S(1)}, u32[]{:S(2)}, u32[]{:S(2)}) collective-permute-start(f32[2,32,128]{2,1,0:T(8,128)S(1)} %maximum_add_fusion.3), channel_id=1, source_target_pairs={{0,64},{2,66},{4,68},{6,70},{8,72},{10,74},{12,76},{14,78},{16,80}... | collective-permute-start | bytes 98312 | tf_op jit(solution)/shard_map/ppermute | solution.py:227
  22.4 1.8 %collective-permute-done.5 = f32[2,32,128]{2,1,0:T(8,128)S(1)} collective-permute-done((f32[2,32,128]{2,1,0:T(8,128)S(1)}, f32[2,32,128]{2,1,0:T(8,128)S(1)}, u32[]{:S(2)}, u32[]{:S(2)}) %collective-permute-start.5) | collective-permute-done | bytes 32800 | tf_op jit(solution)/shard_map/ppermute | solution.py:227
  24.2 2.3 %collective-permute-start.6 = (f32[2,32,128]{2,1,0:T(8,128)S(1)}, f32[2,32,128]{2,1,0:T(8,128)S(1)}, u32[]{:S(2)}, u32[]{:S(2)}) collective-permute-start(f32[2,32,128]{2,1,0:T(8,128)S(1)} %maximum_add_fusion.4), channel_id=1, source_target_pairs={{0,192},{2,194},{4,196},{6,198},{8,200},{10,202},{12,204},{14,206}... | collective-permute-start | bytes 98312 | tf_op jit(solution)/shard_map/ppermute | solution.py:227
  26.5 1.7 %collective-permute-done.6 = f32[2,32,128]{2,1,0:T(8,128)S(1)} collective-permute-done((f32[2,32,128]{2,1,0:T(8,128)S(1)}, f32[2,32,128]{2,1,0:T(8,128)S(1)}, u32[]{:S(2)}, u32[]{:S(2)}) %collective-permute-start.6) | collective-permute-done | bytes 32800 | tf_op jit(solution)/shard_map/ppermute | solution.py:227
  28.4 5.7 %collective-permute-start.7 = (f32[2,32,128]{2,1,0:T(8,128)S(1)}, f32[2,32,128]{2,1,0:T(8,128)S(1)}, u32[]{:S(2)}, u32[]{:S(2)}) collective-permute-start(f32[2,32,128]{2,1,0:T(8,128)S(1)} %get-tuple-element.81), channel_id=1, source_target_pairs={{0,2},{2,0},{4,6},{6,4},{8,10},{10,8},{12,14},{14,12},{16,18},{18,... | collective-permute-start | bytes 98312 | tf_op jit(solution)/shard_map/ppermute | solution.py:272
  34.1 0.8 %own_half.1.base_ref = f32[256,128]{1,0:T(8,128)S(1)} custom-call(f32[2,32,128]{2,1,0:T(8,128)S(1)} %get-tuple-element.80.carry_ref, f32[2,64,128]{2,1,0:T(8,128)S(1)} %get-tuple-element.50.amp_ref, f32[2,16,64,128]{3,2,1,0:T(8,128)S(1)} %get-tuple-element.51.table_ref, f32[2,64,128]{2,1,0:T(8,128)S(1)} %get-tuple-element.52.jump_ref, ...), custom_call_target="tpu_custom_call" | custom-call | tf_op jit(solution)/shard_map/own_half/pallas_call | solution.py:273
  34.9 0.1 collective-permute-done.7.carry_ref
  35.0 1.1 %other_half.1 = (f32[256,128]{1,0:T(8,128)S(1)}, f32[2,256]{1,0:T(2,128)S(1)}) custom-call(f32[2,32,128]{2,1,0:T(8,128)S(1)} %collective-permute-done.7.carry_ref, f32[2,64,128]{2,1,0:T(8,128)S(1)} %get-tuple-element.50.amp_ref, f32[2,16,64,128]{3,2,1,0:T(8,128)S(1)} %get-tuple-element.51.table_ref, f32[2,64,128]{2,1,0:T(8,128)S(1)} %get-tuple-element.52.jump_ref, ...), custom_call_target="tpu_custom_call" | custom-call | tf_op jit(solution)/shard_map/other_half/pallas_call | solution.py:277
  36.1 5.7 %collective-permute-start.8 = (f32[2,256]{1,0:T(2,128)S(1)}, f32[2,256]{1,0:T(2,128)S(1)}, u32[]{:S(2)}, u32[]{:S(2)}) collective-permute-start(f32[2,256]{1,0:T(2,128)S(1)} %get-tuple-element.57.refs_1_), channel_id=1, source_target_pairs={{0,1},{1,0},{2,3},{3,2},{4,5},{5,4},{6,7},{7,6},{8,9},{9,8},{10,11... | collective-permute-start | bytes 6152 | tf_op jit(solution)/shard_map/ppermute | solution.py:283
  41.8 1.0 %collective-permute-done.8.refs_2_ = f32[2,256]{1,0:T(2,128)S(1)} collective-permute-done((f32[2,256]{1,0:T(2,128)S(1)}, f32[2,256]{1,0:T(2,128)S(1)}, u32[]{:S(2)}, u32[]{:S(2)}) %collective-permute-start.8) | collective-permute-done | bytes 2080 | tf_op jit(solution)/shard_map/ppermute | solution.py:283
  42.7 0.9 %norm.1 = f32[256,128]{1,0:T(8,128)} custom-call(f32[256,128]{1,0:T(8,128)S(1)} %get-tuple-element.56.refs_0_, f32[2,256]{1,0:T(2,128)S(1)} %get-tuple-element.57.refs_1_, f32[2,256]{1,0:T(2,128)S(1)} %collective-permute-done.8.refs_2_, f32[1,128]{1,0:T(1,128)S(1)} %get-tuple-element.58.refs_3_), custom_call_target="tpu_custom_call" | custom-call | tf_op jit(solution)/shard_map/norm/pallas_call | solution.py:284
  (23 shorter events, 0.3 us)
Async XLA Ops:
  0.0 5.6 %collective-permute-start = (f32[256,128]{1,0:T(8,128)}, f32[256,128]{1,0:T(8,128)S(1)}, u32[]{:S(2)}, u32[]{:S(2)}) collective-permute-start(f32[256,128]{1,0:T(8,128)} %x_hbm.1), channel_id=1, source_target_pairs={{0,2},{2,0},{4,6},{6,4},{8,10},{10,8},{12,14},{14,12},{16,18},{18,... | collective-permute-start | bytes 393224 | tf_op jit(solution)/shard_map/ppermute | solution.py:203
  6.3 2.9 %collective-permute-start.1 = (f32[2,32,128]{2,1,0:T(8,128)S(1)}, f32[2,32,128]{2,1,0:T(8,128)S(1)}, u32[]{:S(2)}, u32[]{:S(2)}) collective-permute-start(f32[2,32,128]{2,1,0:T(8,128)S(1)} %get-tuple-element.38), channel_id=1, source_target_pairs={{0,4},{2,6},{4,0},{6,2},{8,12},{10,14},{12,8},{14,10},{16,20},{18,... | collective-permute-start | bytes 98312 | tf_op jit(solution)/shard_map/ppermute | solution.py:227
  9.2 4.1 %collective-permute-start.2 = (f32[2,32,128]{2,1,0:T(8,128)S(1)}, f32[2,32,128]{2,1,0:T(8,128)S(1)}, u32[]{:S(2)}, u32[]{:S(2)}) collective-permute-start(f32[2,32,128]{2,1,0:T(8,128)S(1)} %maximum_add_fusion), channel_id=1, source_target_pairs={{0,12},{2,14},{4,8},{6,10},{8,4},{10,6},{12,0},{14,2},{16,28},{18,... | collective-permute-start | bytes 98312 | tf_op jit(solution)/shard_map/ppermute | solution.py:227
  13.3 2.9 %collective-permute-start.3 = (f32[2,32,128]{2,1,0:T(8,128)S(1)}, f32[2,32,128]{2,1,0:T(8,128)S(1)}, u32[]{:S(2)}, u32[]{:S(2)}) collective-permute-start(f32[2,32,128]{2,1,0:T(8,128)S(1)} %maximum_add_fusion.1), channel_id=1, source_target_pairs={{0,16},{2,18},{4,20},{6,22},{8,24},{10,26},{12,28},{14,30},{16,0},... | collective-permute-start | bytes 98312 | tf_op jit(solution)/shard_map/ppermute | solution.py:227
  16.2 4.8 %collective-permute-start.4 = (f32[2,32,128]{2,1,0:T(8,128)S(1)}, f32[2,32,128]{2,1,0:T(8,128)S(1)}, u32[]{:S(2)}, u32[]{:S(2)}) collective-permute-start(f32[2,32,128]{2,1,0:T(8,128)S(1)} %maximum_add_fusion.2), channel_id=1, source_target_pairs={{0,32},{2,34},{4,36},{6,38},{8,40},{10,42},{12,44},{14,46},{16,48}... | collective-permute-start | bytes 98312 | tf_op jit(solution)/shard_map/ppermute | solution.py:227
  21.1 3.1 %collective-permute-start.5 = (f32[2,32,128]{2,1,0:T(8,128)S(1)}, f32[2,32,128]{2,1,0:T(8,128)S(1)}, u32[]{:S(2)}, u32[]{:S(2)}) collective-permute-start(f32[2,32,128]{2,1,0:T(8,128)S(1)} %maximum_add_fusion.3), channel_id=1, source_target_pairs={{0,64},{2,66},{4,68},{6,70},{8,72},{10,74},{12,76},{14,78},{16,80}... | collective-permute-start | bytes 98312 | tf_op jit(solution)/shard_map/ppermute | solution.py:227
  24.2 4.1 %collective-permute-start.6 = (f32[2,32,128]{2,1,0:T(8,128)S(1)}, f32[2,32,128]{2,1,0:T(8,128)S(1)}, u32[]{:S(2)}, u32[]{:S(2)}) collective-permute-start(f32[2,32,128]{2,1,0:T(8,128)S(1)} %maximum_add_fusion.4), channel_id=1, source_target_pairs={{0,192},{2,194},{4,196},{6,198},{8,200},{10,202},{12,204},{14,206}... | collective-permute-start | bytes 98312 | tf_op jit(solution)/shard_map/ppermute | solution.py:227
  28.4 6.5 %collective-permute-start.7 = (f32[2,32,128]{2,1,0:T(8,128)S(1)}, f32[2,32,128]{2,1,0:T(8,128)S(1)}, u32[]{:S(2)}, u32[]{:S(2)}) collective-permute-start(f32[2,32,128]{2,1,0:T(8,128)S(1)} %get-tuple-element.81), channel_id=1, source_target_pairs={{0,2},{2,0},{4,6},{6,4},{8,10},{10,8},{12,14},{14,12},{16,18},{18,... | collective-permute-start | bytes 98312 | tf_op jit(solution)/shard_map/ppermute | solution.py:272
  36.1 6.7 %collective-permute-start.8 = (f32[2,256]{1,0:T(2,128)S(1)}, f32[2,256]{1,0:T(2,128)S(1)}, u32[]{:S(2)}, u32[]{:S(2)}) collective-permute-start(f32[2,256]{1,0:T(2,128)S(1)} %get-tuple-element.57.refs_1_), channel_id=1, source_target_pairs={{0,1},{1,0},{2,3},{3,2},{4,5},{5,4},{6,7},{7,6},{8,9},{9,8},{10,11... | collective-permute-start | bytes 6152 | tf_op jit(solution)/shard_map/ppermute | solution.py:283

commit v2 on v1

--- a/solution.py
+++ b/solution.py
@@ -7,6 +7,7 @@
 
 RADIX = 16
 PRECISE = lax.Precision.HIGHEST
+PARTNERS = (3, 7, 9, 17, 33, 97)
 
 
 def wave(decay, freq, steps):
@@ -44,20 +45,27 @@
 
 
 def half_of_modes(modes, other=0):
-    half = modes // 2
-    return pl.ds(pl.multiple_of((lax.axis_index("seq") % 2 + other) % 2 * half, half), half)
-
-
-def own_state_kernel(x_hbm, decay_ref, freq_ref, state_ref, x_ref, table_ref, jump_ref, block_ref, arrived):
-    copy = pltpu.make_async_copy(x_hbm, x_ref, arrived)
-    copy.start()
+    half, own = modes // 2, lax.axis_index("seq")
+    mine = (own ^ (own >> 1) ^ (own >> 3) ^ (own >> 4) ^ (own >> 5) ^ other) & 1
+    return pl.ds(pl.multiple_of(mine * half, half), half)
+
+
+def own_state_kernel(
+    x_hbm, decay_hbm, freq_hbm, state_ref, x_ref, decay_ref, freq_ref, table_ref, jump_ref, block_ref, arrived
+):
+    sources, targets = (decay_hbm, freq_hbm, x_hbm), (decay_ref, freq_ref, x_ref)
+    copies = [pltpu.make_async_copy(s, t, arrived.at[i]) for i, (s, t) in enumerate(zip(sources, targets))]
+    for copy in copies:
+        copy.start()
+    copies[0].wait()
+    copies[1].wait()
     mine = half_of_modes(decay_ref.shape[0])
     decay, freq = decay_ref[mine, :], freq_ref[mine, :]
     zr, zi = wave(decay, freq, 1)
     jump_ref[0], jump_ref[1] = wave(decay, freq, RADIX)
     block_ref[0], block_ref[1] = wave(decay, freq, x_ref.shape[0])
     fill_powers(table_ref, zr, zi)
-    copy.wait()
+    copies[2].wait()
     state_ref[0], state_ref[1] = reduced(x_ref, table_ref, jump_ref)
 
 
@@ -105,16 +113,19 @@
     return total
 
 
-def taps_kernel(decay_ref, freq_ref, real_ref, imag_ref, gain_in, taps_ref, amp_ref, table_ref, jump_ref, gain_ref, partial):
-    rows, modes = taps_ref.shape[0], decay_ref.shape[0]
+def tables_kernel(decay_ref, freq_ref, real_ref, imag_ref, gain_in, amp_ref, next_ref, table_ref, jump_ref, gain_ref):
     gain_ref[...] = gain_in[...]
     scale = 2.0 * jnp.sqrt(decay_ref[...])
-    ar, ai = scale * real_ref[...], scale * imag_ref[...]
+    amp_ref[0], amp_ref[1] = scale * real_ref[...], scale * imag_ref[...]
     zr, zi = wave(decay_ref[...], freq_ref[...], 1)
     jump_ref[0], jump_ref[1] = wave(decay_ref[...], freq_ref[...], RADIX)
-    amp_ref[0], amp_ref[1] = times(ar, ai, zr, zi)
+    next_ref[0], next_ref[1] = times(amp_ref[0], amp_ref[1], zr, zi)
     fill_powers(table_ref, zr, zi)
-    expand(ar, ai, table_ref, jump_ref, pl.ds(0, modes), partial, rows)
+
+
+def taps_kernel(amp_ref, table_ref, jump_ref, taps_ref, partial):
+    rows, modes = taps_ref.shape[0], amp_ref.shape[1]
+    expand(amp_ref[0], amp_ref[1], table_ref, jump_ref, pl.ds(0, modes), partial, rows)
     for g in range(rows // 8):
         taps_ref[8 * g : 8 * g + 8, :] = gathered(partial, g)
 
@@ -201,17 +212,19 @@
     core_pairs = [(i, i ^ 1) for i in range(shards)]
 
     other_x = lax.ppermute(signal, "seq", core_pairs)
-    state, x, own_table, own_jump, block = pl.pallas_call(
+    state, x, near_decay, near_freq, own_table, own_jump, block = pl.pallas_call(
         own_state_kernel,
-        in_specs=[pl.BlockSpec(memory_space=pl.ANY), pl.BlockSpec(), pl.BlockSpec()],
+        in_specs=[pl.BlockSpec(memory_space=pl.ANY)] * 3,
         out_shape=(
             vmem(2, half, lanes),
             vmem(rows, lanes),
+            vmem(modes, lanes),
+            vmem(modes, lanes),
             vmem(2, RADIX, half, lanes),
             vmem(2, half, lanes),
             vmem(2, half, lanes),
         ),
-        scratch_shapes=[pltpu.SemaphoreType.DMA],
+        scratch_shapes=[pltpu.SemaphoreType.DMA((3,))],
         name="own_state",
     )(signal, decay, freq)
     other_x, state = lax.optimization_barrier((other_x, state))
@@ -219,33 +232,36 @@
         chip_state_kernel, out_shape=(vmem(2, half, lanes), vmem(2, half, lanes)), name="chip_state"
     )(near(other_x), near(own_table), near(own_jump), near(block), near(state))
 
-    partners = (2, 6, 8, 16, 32, 96)
     carry = jnp.zeros_like(total)
     power_r, power_i = jnp.ones((half, lanes), jnp.float32), jnp.zeros((half, lanes), jnp.float32)
     powers = taps = local = late = None
-    for k, partner in enumerate(partners):
+    for k, partner in enumerate(PARTNERS):
         late = lax.ppermute(total, "seq", [(i, i ^ partner) for i in range(shards)])
         upper = (own >> (k + 1)) & 1 == 1
         if k == 0:
             powers = pl.pallas_call(
                 lambda *refs: chip_powers_kernel(*refs, rows=rows),
-                out_shape=vmem(len(partners), 2, half, lanes),
+                out_shape=vmem(len(PARTNERS), 2, half, lanes),
                 name="chip_powers",
-            )(near(after(block, total)), decay, freq)
+            )(near(after(block, total)), near(near_decay), near(near_freq))
             late, powers = lax.optimization_barrier((late, powers))
         if k == 1:
-            taps, amp, table, jump, gain = pl.pallas_call(
-                taps_kernel,
+            amp, next_amp, table, jump, gain = pl.pallas_call(
+                tables_kernel,
                 out_shape=(
-                    vmem(rows, lanes),
+                    vmem(2, modes, lanes),
                     vmem(2, modes, lanes),
                     vmem(2, RADIX, modes, lanes),
                     vmem(2, modes, lanes),
                     vmem(1, lanes),
                 ),
-                scratch_shapes=[partial],
-                name="taps",
-            )(after(decay, total), freq, real, imag, gain)
+                name="tables",
+            )(near(after(near_decay, total)), near(near_freq), real, imag, gain)
+            late, amp = lax.optimization_barrier((late, amp))
+        if k == 2:
+            taps = pl.pallas_call(taps_kernel, out_shape=vmem(rows, lanes), scratch_shapes=[partial], name="taps")(
+                near(after(amp, total)), near(table), near(jump)
+            )
             late, taps = lax.optimization_barrier((late, taps))
         if k == 3:
             local = pl.pallas_call(
@@ -257,7 +273,7 @@
             late, local = lax.optimization_barrier((late, local))
         add_r, add_i = times(power_r, power_i, late[0], late[1])
         carry = carry + jnp.where(upper, jnp.stack([add_r, add_i]), 0.0)
-        if k + 1 == len(partners):
+        if k + 1 == len(PARTNERS):
             break
         wr, wi = powers[k, 0], powers[k, 1]
         low, high = jnp.where(upper, late, total), jnp.where(upper, total, late)
@@ -271,7 +287,7 @@
     own_carry, other_carry = jnp.where(odd, second, carry), jnp.where(odd, carry, second)
     other_carry = lax.ppermute(other_carry, "seq", core_pairs)
     part = pl.pallas_call(own_half_kernel, out_shape=vmem(rows, lanes), scratch_shapes=[partial], name="own_half")(
-        near(own_carry), near(amp), near(table), near(jump), near(local)
+        near(own_carry), near(next_amp), near(table), near(jump), near(local)
     )
     other_carry, part = lax.optimization_barrier((other_carry, part))
     summed, stats = pl.pallas_call(
@@ -279,7 +295,7 @@
         out_shape=(vmem(rows, lanes), vmem(2, rows)),
         scratch_shapes=[partial],
         name="other_half",
-    )(near(other_carry), near(amp), near(table), near(jump), near(part))
+    )(near(other_carry), near(next_amp), near(table), near(jump), near(part))
     other = lax.ppermute(stats, "ch", [(0, 1), (1, 0)])
     return pl.pallas_call(
         lambda *refs: norm_kernel(*refs, channels=channels),

time: 43.9 us -> 40.2 us (0.916)
  starting transfers between devices: 23.7 us -> 13.1 us
  waiting for transfers between devices: 8.25 us -> 16.7 us
  Pallas kernels: 11.2 us -> 9.78 us
    ppermute x6, waiting for transfers between devices: 7.22 us -> 15.3 us  [on_device(): late = lax.ppermute(total, 'seq', [(i, i ^ partner) for i in range(shards)])]
    ppermute x1, starting transfers between devices: 5.67 us -> 0.09 us  [on_device(): other_carry = lax.ppermute(other_carry, 'seq', core_pairs)]
    ppermute x6, starting transfers between devices: 9.12 us -> 4.35 us  [on_device(): late = lax.ppermute(total, 'seq', [(i, i ^ partner) for i in range(shards)])]
    pallas_call x1, Pallas kernels: 0.87 us -> 0.09 us  [on_device(): pl.pallas_call(lambda *refs: chip_powers_kernel(*refs, rows=rows), out_sh...]
    pallas_call x1, Pallas kernels: 2.37 us -> 1.72 us  [on_device(): pl.pallas_call(own_state_kernel, in_specs=[pl.BlockSpec(memory_space=pl.A...]
    pallas_call x1 -> x2, Pallas kernels: 2.57 us -> 2.54 us  [the longest x1 1.4 us: on_device(): pl.pallas_call(taps_kernel, out_shape=vmem(rows, lanes), scratch_shapes=[...]
  transfers between devices with their start and end apart: 9 -> 9, of which waited for: 7 -> 8; matrix products, arithmetic and copies ran while one was open for 0% -> 0% of each run, Pallas kernels for 20% -> 18%
where the time goes in v2:
time: 40.2 us; the launch traced here: 40 us
  waiting for transfers between devices  16.7 us (42%)
  starting transfers between devices  13.1 us (33%)
  Pallas kernels  9.78 us (24%)
    ppermute x6, waiting for transfers between devices, on_device(): late = lax.ppermute(total, 'seq', [(i, i ^ partner) for i in range(shards)])  15.3 us
    ppermute x1, starting transfers between devices, on_device(): other = lax.ppermute(stats, 'ch', [(0, 1), (1, 0)])  5.46 us
    ppermute x6, starting transfers between devices, on_device(): late = lax.ppermute(total, 'seq', [(i, i ^ partner) for i in range(shards)])  4.35 us
    ppermute x1, starting transfers between devices, on_device(): other_x = lax.ppermute(signal, 'seq', core_pairs)  3.2 us
    pallas_call x1, Pallas kernels, on_device(): pl.pallas_call(local_kernel, out_shape=vmem(rows, lanes), scratch_shapes=...  1.93 us
    pallas_call x1, Pallas kernels, on_device(): pl.pallas_call(own_state_kernel, in_specs=[pl.BlockSpec(memory_space=pl.A...  1.72 us
    pallas_call x1, Pallas kernels, on_device(): pl.pallas_call(taps_kernel, out_shape=vmem(rows, lanes), scratch_shapes=[...  1.4 us
    pallas_call x1, Pallas kernels, on_device(): pl.pallas_call(tables_kernel, out_shape=(vmem(2, modes, lanes), vmem(2, m...  1.14 us
  transfers between devices with their start and end apart: 9, of which 8 were waited for; matrix products, arithmetic and copies ran while one was open for 0% of the time, Pallas kernels for 18%

profile of v2, /device:TPU:1, one launch (start us, length us, event | category | flops | bytes accessed | tf_op | source)
XLA Modules:
  0.0 40.0 jit_solution(13340931325538303230)
XLA Ops:
  0.0 3.2 %collective-permute-start = (f32[256,128]{1,0:T(8,128)}, f32[256,128]{1,0:T(8,128)S(1)}, u32[]{:S(2)}, u32[]{:S(2)}) collective-permute-start(f32[256,128]{1,0:T(8,128)} %x_hbm.1), channel_id=1, source_target_pairs={{0,2},{2,0},{4,6},{6,4},{8,10},{10,8},{12,14},{14,12},{16,18},{18,... | collective-permute-start | bytes 393224 | tf_op jit(solution)/shard_map/ppermute | solution.py:214
  3.2 1.7 %own_state.1 = (f32[2,32,128]{2,1,0:T(8,128)S(1)}, f32[256,128]{1,0:T(8,128)S(1)}, f32[64,128]{1,0:T(8,128)S(1)}, f32[64,128]{1,0:T(8,128)S(1)}, f32[2,16,32,128...) custom-call(f32[256,128]{1,0:T(8,128)} %x_hbm.1, f32[64,128]{1,0:T(8,128)} %bitcast.172, ...), custom_call_target="tpu_custom_call" | custom-call | tf_op jit(solution)/shard_map/own_state/pallas_call | solution.py:215
  4.9 0.0 collective-permute-done.x_ref
  4.9 0.7 %chip_state.1 = (f32[2,32,128]{2,1,0:T(8,128)S(1)}, f32[2,32,128]{2,1,0:T(8,128)S(1)}) custom-call(f32[256,128]{1,0:T(8,128)S(1)} %collective-permute-done.x_ref, f32[2,16,32,128]{3,2,1,0:T(8,128)S(1)} %get-tuple-element.39.table_ref, f32[2,32,128]{2,1,0:T(8,128)S(1)} %get-tuple-element.40.jump_ref, f32[2,32,128]{2,1,0:T(8,128)S(1)} %get-tuple-element.44.block_ref.refs_0_, ...), custom_call_target="tpu_custom_call" | custom-call | tf_op jit(solution)/shard_map/chip_state/pallas_call | solution.py:231
  5.7 0.1 collective-permute-start.1
  5.8 0.1 chip_powers.1
  5.9 3.2 %collective-permute-done.1 = f32[2,32,128]{2,1,0:T(8,128)S(1)} collective-permute-done((f32[2,32,128]{2,1,0:T(8,128)S(1)}, f32[2,32,128]{2,1,0:T(8,128)S(1)}, u32[]{:S(2)}, u32[]{:S(2)}) %collective-permute-start.1) | collective-permute-done | bytes 32800 | tf_op jit(solution)/shard_map/ppermute | solution.py:239
  9.1 1.0 %collective-permute-start.2 = (f32[2,32,128]{2,1,0:T(8,128)S(1)}, f32[2,32,128]{2,1,0:T(8,128)S(1)}, u32[]{:S(2)}, u32[]{:S(2)}) collective-permute-start(f32[2,32,128]{2,1,0:T(8,128)S(1)} %maximum_add_fusion), channel_id=1, source_target_pairs={{0,14},{2,12},{4,10},{6,8},{8,6},{10,4},{12,2},{14,0},{16,30},{18,... | collective-permute-start | bytes 98312 | tf_op jit(solution)/shard_map/ppermute | solution.py:239
  10.1 1.1 %tables.1 = (f32[2,64,128]{2,1,0:T(8,128)S(1)}, f32[2,64,128]{2,1,0:T(8,128)S(1)}, f32[2,16,64,128]{3,2,1,0:T(8,128)S(1)}, f32[2,64,128]{2,1,0:T(8,128)S(1)}, f32[1,128]{1,0:T(1,128)S(1)}) custom-call(f32[64,128]{1,0:T(8,128)S(1)} %get-tuple-element.49.refs_1_.decay_ref, f32[64,128]{1,0:T(8,128)S(1)} %get-tuple-element.46.refs_2_.freq_ref, ...), custom_call_target="tpu_custom_call" | custom-call | tf_op jit(solution)/shard_map/tables/pallas_call | solution.py:249
  11.3 2.5 %collective-permute-done.2 = f32[2,32,128]{2,1,0:T(8,128)S(1)} collective-permute-done((f32[2,32,128]{2,1,0:T(8,128)S(1)}, f32[2,32,128]{2,1,0:T(8,128)S(1)}, u32[]{:S(2)}, u32[]{:S(2)}) %collective-permute-start.2) | collective-permute-done | bytes 32800 | tf_op jit(solution)/shard_map/ppermute | solution.py:239
  13.8 0.1 collective-permute-start.3
  13.9 1.4 %taps.1.taps_ref = f32[256,128]{1,0:T(8,128)S(1)} custom-call(f32[2,64,128]{2,1,0:T(8,128)S(1)} %get-tuple-element.53.amp_ref, f32[2,16,64,128]{3,2,1,0:T(8,128)S(1)} %get-tuple-element.54.table_ref, f32[2,64,128]{2,1,0:T(8,128)S(1)} %get-tuple-element.55.jump_ref), custom_call_target="tpu_custom_call" | custom-call | tf_op jit(solution)/shard_map/taps/pallas_call | solution.py:262
  15.3 1.9 %collective-permute-done.3 = f32[2,32,128]{2,1,0:T(8,128)S(1)} collective-permute-done((f32[2,32,128]{2,1,0:T(8,128)S(1)}, f32[2,32,128]{2,1,0:T(8,128)S(1)}, u32[]{:S(2)}, u32[]{:S(2)}) %collective-permute-start.3) | collective-permute-done | bytes 32800 | tf_op jit(solution)/shard_map/ppermute | solution.py:239
  17.3 1.5 %collective-permute-start.4 = (f32[2,32,128]{2,1,0:T(8,128)S(1)}, f32[2,32,128]{2,1,0:T(8,128)S(1)}, u32[]{:S(2)}, u32[]{:S(2)}) collective-permute-start(f32[2,32,128]{2,1,0:T(8,128)S(1)} %maximum_add_fusion.2), channel_id=1, source_target_pairs={{0,34},{2,32},{4,38},{6,36},{8,42},{10,40},{12,46},{14,44},{16,50}... | collective-permute-start | bytes 98312 | tf_op jit(solution)/shard_map/ppermute | solution.py:239
  18.8 1.9 %local.1.base_ref = f32[256,128]{1,0:T(8,128)S(1)} custom-call(f32[256,128]{1,0:T(8,128)S(1)} %get-tuple-element.58.x_ref, f32[256,128]{1,0:T(8,128)S(1)} %taps.1.taps_ref, f32[1,128]{1,0:T(1,128)} %bitcast.177), custom_call_target="tpu_custom_call" | custom-call | tf_op jit(solution)/shard_map/local/pallas_call | solution.py:267
  20.7 1.3 %collective-permute-done.4 = f32[2,32,128]{2,1,0:T(8,128)S(1)} collective-permute-done((f32[2,32,128]{2,1,0:T(8,128)S(1)}, f32[2,32,128]{2,1,0:T(8,128)S(1)}, u32[]{:S(2)}, u32[]{:S(2)}) %collective-permute-start.4) | collective-permute-done | bytes 32800 | tf_op jit(solution)/shard_map/ppermute | solution.py:239
  22.0 0.2 collective-permute-start.5
  22.2 3.3 %collective-permute-done.5 = f32[2,32,128]{2,1,0:T(8,128)S(1)} collective-permute-done((f32[2,32,128]{2,1,0:T(8,128)S(1)}, f32[2,32,128]{2,1,0:T(8,128)S(1)}, u32[]{:S(2)}, u32[]{:S(2)}) %collective-permute-start.5) | collective-permute-done | bytes 32800 | tf_op jit(solution)/shard_map/ppermute | solution.py:239
  25.5 1.4 %collective-permute-start.6 = (f32[2,32,128]{2,1,0:T(8,128)S(1)}, f32[2,32,128]{2,1,0:T(8,128)S(1)}, u32[]{:S(2)}, u32[]{:S(2)}) collective-permute-start(f32[2,32,128]{2,1,0:T(8,128)S(1)} %maximum_add_fusion.4), channel_id=1, source_target_pairs={{0,194},{2,192},{4,198},{6,196},{8,202},{10,200},{12,206},{14,204}... | collective-permute-start | bytes 98312 | tf_op jit(solution)/shard_map/ppermute | solution.py:239
  26.9 3.2 %collective-permute-done.6 = f32[2,32,128]{2,1,0:T(8,128)S(1)} collective-permute-done((f32[2,32,128]{2,1,0:T(8,128)S(1)}, f32[2,32,128]{2,1,0:T(8,128)S(1)}, u32[]{:S(2)}, u32[]{:S(2)}) %collective-permute-start.6) | collective-permute-done | bytes 32800 | tf_op jit(solution)/shard_map/ppermute | solution.py:239
  30.3 0.1 collective-permute-start.7
  30.4 0.8 %own_half.1.base_ref = f32[256,128]{1,0:T(8,128)S(1)} custom-call(f32[2,32,128]{2,1,0:T(8,128)S(1)} %get-tuple-element.90.carry_ref, f32[2,64,128]{2,1,0:T(8,128)S(1)} %get-tuple-element.62.amp_ref, f32[2,16,64,128]{3,2,1,0:T(8,128)S(1)} %get-tuple-element.54.table_ref, f32[2,64,128]{2,1,0:T(8,128)S(1)} %get-tuple-element.55.jump_ref, ...), custom_call_target="tpu_custom_call" | custom-call | tf_op jit(solution)/shard_map/own_half/pallas_call | solution.py:289
  31.2 0.4 collective-permute-done.7.carry_ref
  31.6 1.1 %other_half.1 = (f32[256,128]{1,0:T(8,128)S(1)}, f32[2,256]{1,0:T(2,128)S(1)}) custom-call(f32[2,32,128]{2,1,0:T(8,128)S(1)} %collective-permute-done.7.carry_ref, f32[2,64,128]{2,1,0:T(8,128)S(1)} %get-tuple-element.62.amp_ref, f32[2,16,64,128]{3,2,1,0:T(8,128)S(1)} %get-tuple-element.54.table_ref, f32[2,64,128]{2,1,0:T(8,128)S(1)} %get-tuple-element.55.jump_ref, ...), custom_call_target="tpu_custom_call" | custom-call | tf_op jit(solution)/shard_map/other_half/pallas_call | solution.py:293
  32.7 5.5 %collective-permute-start.8 = (f32[2,256]{1,0:T(2,128)S(1)}, f32[2,256]{1,0:T(2,128)S(1)}, u32[]{:S(2)}, u32[]{:S(2)}) collective-permute-start(f32[2,256]{1,0:T(2,128)S(1)} %get-tuple-element.67.refs_1_), channel_id=1, source_target_pairs={{0,1},{1,0},{2,3},{3,2},{4,5},{5,4},{6,7},{7,6},{8,9},{9,8},{10,11... | collective-permute-start | bytes 6152 | tf_op jit(solution)/shard_map/ppermute | solution.py:299
  38.2 1.0 %collective-permute-done.8.refs_2_ = f32[2,256]{1,0:T(2,128)S(1)} collective-permute-done((f32[2,256]{1,0:T(2,128)S(1)}, f32[2,256]{1,0:T(2,128)S(1)}, u32[]{:S(2)}, u32[]{:S(2)}) %collective-permute-start.8) | collective-permute-done | bytes 2080 | tf_op jit(solution)/shard_map/ppermute | solution.py:299
  39.1 0.9 %norm.1 = f32[256,128]{1,0:T(8,128)} custom-call(f32[256,128]{1,0:T(8,128)S(1)} %get-tuple-element.66.refs_0_, f32[2,256]{1,0:T(2,128)S(1)} %get-tuple-element.67.refs_1_, f32[2,256]{1,0:T(2,128)S(1)} %collective-permute-done.8.refs_2_, f32[1,128]{1,0:T(1,128)S(1)} %get-tuple-element.68.refs_3_), custom_call_target="tpu_custom_call" | custom-call | tf_op jit(solution)/shard_map/norm/pallas_call | solution.py:300
  (23 shorter events, 0.3 us)
Async XLA Ops:
  0.0 4.9 %collective-permute-start = (f32[256,128]{1,0:T(8,128)}, f32[256,128]{1,0:T(8,128)S(1)}, u32[]{:S(2)}, u32[]{:S(2)}) collective-permute-start(f32[256,128]{1,0:T(8,128)} %x_hbm.1), channel_id=1, source_target_pairs={{0,2},{2,0},{4,6},{6,4},{8,10},{10,8},{12,14},{14,12},{16,18},{18,... | collective-permute-start | bytes 393224 | tf_op jit(solution)/shard_map/ppermute | solution.py:214
  5.7 3.4 %collective-permute-start.1 = (f32[2,32,128]{2,1,0:T(8,128)S(1)}, f32[2,32,128]{2,1,0:T(8,128)S(1)}, u32[]{:S(2)}, u32[]{:S(2)}) collective-permute-start(f32[2,32,128]{2,1,0:T(8,128)S(1)} %get-tuple-element.43), channel_id=1, source_target_pairs={{0,6},{2,4},{4,2},{6,0},{8,14},{10,12},{12,10},{14,8},{16,22},{18,... | collective-permute-start | bytes 98312 | tf_op jit(solution)/shard_map/ppermute | solution.py:239
  9.1 4.6 %collective-permute-start.2 = (f32[2,32,128]{2,1,0:T(8,128)S(1)}, f32[2,32,128]{2,1,0:T(8,128)S(1)}, u32[]{:S(2)}, u32[]{:S(2)}) collective-permute-start(f32[2,32,128]{2,1,0:T(8,128)S(1)} %maximum_add_fusion), channel_id=1, source_target_pairs={{0,14},{2,12},{4,10},{6,8},{8,6},{10,4},{12,2},{14,0},{16,30},{18,... | collective-permute-start | bytes 98312 | tf_op jit(solution)/shard_map/ppermute | solution.py:239
  13.8 3.4 %collective-permute-start.3 = (f32[2,32,128]{2,1,0:T(8,128)S(1)}, f32[2,32,128]{2,1,0:T(8,128)S(1)}, u32[]{:S(2)}, u32[]{:S(2)}) collective-permute-start(f32[2,32,128]{2,1,0:T(8,128)S(1)} %maximum_add_fusion.1), channel_id=1, source_target_pairs={{0,18},{2,16},{4,22},{6,20},{8,26},{10,24},{12,30},{14,28},{16,2},... | collective-permute-start | bytes 98312 | tf_op jit(solution)/shard_map/ppermute | solution.py:239
  17.3 4.7 %collective-permute-start.4 = (f32[2,32,128]{2,1,0:T(8,128)S(1)}, f32[2,32,128]{2,1,0:T(8,128)S(1)}, u32[]{:S(2)}, u32[]{:S(2)}) collective-permute-start(f32[2,32,128]{2,1,0:T(8,128)S(1)} %maximum_add_fusion.2), channel_id=1, source_target_pairs={{0,34},{2,32},{4,38},{6,36},{8,42},{10,40},{12,46},{14,44},{16,50}... | collective-permute-start | bytes 98312 | tf_op jit(solution)/shard_map/ppermute | solution.py:239
  22.0 3.4 %collective-permute-start.5 = (f32[2,32,128]{2,1,0:T(8,128)S(1)}, f32[2,32,128]{2,1,0:T(8,128)S(1)}, u32[]{:S(2)}, u32[]{:S(2)}) collective-permute-start(f32[2,32,128]{2,1,0:T(8,128)S(1)} %maximum_add_fusion.3), channel_id=1, source_target_pairs={{0,66},{2,64},{4,70},{6,68},{8,74},{10,72},{12,78},{14,76},{16,82}... | collective-permute-start | bytes 98312 | tf_op jit(solution)/shard_map/ppermute | solution.py:239
  25.5 4.6 %collective-permute-start.6 = (f32[2,32,128]{2,1,0:T(8,128)S(1)}, f32[2,32,128]{2,1,0:T(8,128)S(1)}, u32[]{:S(2)}, u32[]{:S(2)}) collective-permute-start(f32[2,32,128]{2,1,0:T(8,128)S(1)} %maximum_add_fusion.4), channel_id=1, source_target_pairs={{0,194},{2,192},{4,198},{6,196},{8,202},{10,200},{12,206},{14,204}... | collective-permute-start | bytes 98312 | tf_op jit(solution)/shard_map/ppermute | solution.py:239
  30.3 1.3 %collective-permute-start.7 = (f32[2,32,128]{2,1,0:T(8,128)S(1)}, f32[2,32,128]{2,1,0:T(8,128)S(1)}, u32[]{:S(2)}, u32[]{:S(2)}) collective-permute-start(f32[2,32,128]{2,1,0:T(8,128)S(1)} %get-tuple-element.91), channel_id=1, source_target_pairs={{0,2},{2,0},{4,6},{6,4},{8,10},{10,8},{12,14},{14,12},{16,18},{18,... | collective-permute-start | bytes 98312 | tf_op jit(solution)/shard_map/ppermute | solution.py:288
  32.7 6.4 %collective-permute-start.8 = (f32[2,256]{1,0:T(2,128)S(1)}, f32[2,256]{1,0:T(2,128)S(1)}, u32[]{:S(2)}, u32[]{:S(2)}) collective-permute-start(f32[2,256]{1,0:T(2,128)S(1)} %get-tuple-element.67.refs_1_), channel_id=1, source_target_pairs={{0,1},{1,0},{2,3},{3,2},{4,5},{5,4},{6,7},{7,6},{8,9},{9,8},{10,11... | collective-permute-start | bytes 6152 | tf_op jit(solution)/shard_map/ppermute | solution.py:299

commit v3 on v2

--- a/solution.py
+++ b/solution.py
@@ -7,7 +7,7 @@
 
 RADIX = 16
 PRECISE = lax.Precision.HIGHEST
-PARTNERS = (3, 7, 9, 17, 33, 97)
+LEVELS = ((4, 7, 3), (16, 25, 9), (64, 97, 33))
 
 
 def wave(decay, freq, steps):
@@ -46,7 +46,7 @@
 
 def half_of_modes(modes, other=0):
     half, own = modes // 2, lax.axis_index("seq")
-    mine = (own ^ (own >> 1) ^ (own >> 3) ^ (own >> 4) ^ (own >> 5) ^ other) & 1
+    mine = (own ^ (own >> 1) ^ (own >> 3) ^ (own >> 5) ^ other) & 1
     return pl.ds(pl.multiple_of(mine * half, half), half)
 
 
@@ -232,20 +232,18 @@
         chip_state_kernel, out_shape=(vmem(2, half, lanes), vmem(2, half, lanes)), name="chip_state"
     )(near(other_x), near(own_table), near(own_jump), near(block), near(state))
 
-    carry = jnp.zeros_like(total)
-    power_r, power_i = jnp.ones((half, lanes), jnp.float32), jnp.zeros((half, lanes), jnp.float32)
-    powers = taps = local = late = None
-    for k, partner in enumerate(PARTNERS):
-        late = lax.ppermute(total, "seq", [(i, i ^ partner) for i in range(shards)])
-        upper = (own >> (k + 1)) & 1 == 1
-        if k == 0:
+    zero = jnp.zeros((half, lanes), jnp.float32)
+    carry, power = (zero, zero), (zero + 1.0, zero)
+    for level, distances in enumerate(LEVELS):
+        alike, opposite, near_by = (
+            lax.ppermute(total, "seq", [(i, i ^ distance) for i in range(shards)]) for distance in distances
+        )
+        if level == 0:
             powers = pl.pallas_call(
                 lambda *refs: chip_powers_kernel(*refs, rows=rows),
-                out_shape=vmem(len(PARTNERS), 2, half, lanes),
+                out_shape=vmem(2 * len(LEVELS), 2, half, lanes),
                 name="chip_powers",
             )(near(after(block, total)), near(near_decay), near(near_freq))
-            late, powers = lax.optimization_barrier((late, powers))
-        if k == 1:
             amp, next_amp, table, jump, gain = pl.pallas_call(
                 tables_kernel,
                 out_shape=(
@@ -257,31 +255,41 @@
                 ),
                 name="tables",
             )(near(after(near_decay, total)), near(near_freq), real, imag, gain)
-            late, amp = lax.optimization_barrier((late, amp))
-        if k == 2:
+            alike, opposite, near_by, powers, amp = lax.optimization_barrier((alike, opposite, near_by, powers, amp))
+        if level == 1:
             taps = pl.pallas_call(taps_kernel, out_shape=vmem(rows, lanes), scratch_shapes=[partial], name="taps")(
                 near(after(amp, total)), near(table), near(jump)
             )
-            late, taps = lax.optimization_barrier((late, taps))
-        if k == 3:
+            alike, opposite, near_by, taps = lax.optimization_barrier((alike, opposite, near_by, taps))
+        if level == 2:
             local = pl.pallas_call(
                 local_kernel,
                 out_shape=vmem(rows, lanes),
                 scratch_shapes=[vmem(rows + 8, lanes), vmem(8, rows, lanes)],
                 name="local",
             )(near(after(x, total)), near(taps), skip)
-            late, local = lax.optimization_barrier((late, local))
-        add_r, add_i = times(power_r, power_i, late[0], late[1])
-        carry = carry + jnp.where(upper, jnp.stack([add_r, add_i]), 0.0)
-        if k + 1 == len(PARTNERS):
-            break
-        wr, wi = powers[k, 0], powers[k, 1]
-        low, high = jnp.where(upper, late, total), jnp.where(upper, total, late)
-        total = jnp.stack(times(low[0], low[1], wr, wi)) + high
-        next_r, next_i = times(power_r, power_i, wr, wi)
-        power_r = jnp.where(upper, next_r, power_r)
-        power_i = jnp.where(upper, next_i, power_i)
-
+            alike, opposite, near_by, local = lax.optimization_barrier((alike, opposite, near_by, local))
+        second = (own >> (2 * level + 1)) & 1 == 1
+        upper = (own >> (2 * level + 2)) & 1 == 1
+        step, double = powers[2 * level], powers[2 * level + 1]
+
+        def chosen(flag, one, two):
+            return jnp.where(flag, one[0], two[0]), jnp.where(flag, one[1], two[1])
+
+        def plus(one, two):
+            return one[0] + two[0], one[1] + two[1]
+
+        other_pair = plus(times(*chosen(second, opposite, alike), *step), chosen(second, alike, opposite))
+        carry = plus(carry, chosen(second, times(*power, *near_by), (zero, zero)))
+        power = chosen(second, times(*power, *step), power)
+        carry = plus(carry, chosen(upper, times(*power, *other_pair), (zero, zero)))
+        power = chosen(upper, times(*power, *double), power)
+        if level + 1 < len(LEVELS):
+            own_pair = plus(times(*chosen(second, near_by, total), *step), chosen(second, total, near_by))
+            low, high = chosen(upper, other_pair, own_pair), chosen(upper, own_pair, other_pair)
+            total = jnp.stack(plus(times(*low, *double), high))
+
+    carry = jnp.stack(carry)
     odd = own % 2 == 1
     second = jnp.stack(times(carry[0], carry[1], block[0], block[1])) + first
     own_carry, other_carry = jnp.where(odd, second, carry), jnp.where(odd, carry, second)

time: 40.2 us -> 38.3 us (0.953)
  waiting for transfers between devices: 16.7 us -> 7.05 us
  starting transfers between devices: 13.1 us -> 21 us
    ppermute x6 -> x9, waiting for transfers between devices: 15.3 us -> 5.53 us  [on_device(): lax.ppermute(total, 'seq', [(i, i ^ distance) for i in range(shards)])]
    ppermute x6 -> x9, starting transfers between devices: 4.35 us -> 12.4 us  [on_device(): lax.ppermute(total, 'seq', [(i, i ^ distance) for i in range(shards)])]
    ppermute x1, starting transfers between devices: 5.46 us -> 4.91 us  [on_device(): other = lax.ppermute(stats, 'ch', [(0, 1), (1, 0)])]
    ppermute x1, waiting for transfers between devices: 0.97 us -> 1.45 us  [on_device(): other = lax.ppermute(stats, 'ch', [(0, 1), (1, 0)])]
  transfers between devices with their start and end apart: 9 -> 12, of which waited for: 8 -> 7; matrix products, arithmetic and copies ran while one was open for 0% -> 0% of each run, Pallas kernels for 18% -> 19%
where the time goes in v3:
time: 38.3 us; the launch traced here: 38.1 us
  starting transfers between devices  21 us (55%)
  Pallas kernels  9.77 us (26%)
  waiting for transfers between devices  7.05 us (18%)
    ppermute x9, starting transfers between devices, on_device(): lax.ppermute(total, 'seq', [(i, i ^ distance) for i in range(shards)])  12.4 us
    ppermute x9, waiting for transfers between devices, on_device(): lax.ppermute(total, 'seq', [(i, i ^ distance) for i in range(shards)])  5.53 us
    ppermute x1, starting transfers between devices, on_device(): other = lax.ppermute(stats, 'ch', [(0, 1), (1, 0)])  4.91 us
    ppermute x1, starting transfers between devices, on_device(): other_x = lax.ppermute(signal, 'seq', core_pairs)  3.2 us
    pallas_call x1, Pallas kernels, on_device(): pl.pallas_call(local_kernel, out_shape=vmem(rows, lanes), scratch_shapes=...  1.93 us
    pallas_call x1, Pallas kernels, on_device(): pl.pallas_call(own_state_kernel, in_specs=[pl.BlockSpec(memory_space=pl.A...  1.72 us
    ppermute x1, waiting for transfers between devices, on_device(): other = lax.ppermute(stats, 'ch', [(0, 1), (1, 0)])  1.45 us
    pallas_call x1, Pallas kernels, on_device(): pl.pallas_call(taps_kernel, out_shape=vmem(rows, lanes), scratch_shapes=[...  1.4 us
  transfers between devices with their start and end apart: 12, of which 7 were waited for; matrix products, arithmetic and copies ran while one was open for 0% of the time, Pallas kernels for 19%

profile of v3, /device:TPU:1, one launch (start us, length us, event | category | flops | bytes accessed | tf_op | source)
XLA Modules:
  0.0 38.1 jit_solution(6965890771510452225)
XLA Ops:
  0.0 3.2 %collective-permute-start = (f32[256,128]{1,0:T(8,128)}, f32[256,128]{1,0:T(8,128)S(1)}, u32[]{:S(2)}, u32[]{:S(2)}) collective-permute-start(f32[256,128]{1,0:T(8,128)} %x_hbm.1), channel_id=1, source_target_pairs={{0,2},{2,0},{4,6},{6,4},{8,10},{10,8},{12,14},{14,12},{16,18},{18,... | collective-permute-start | bytes 393224 | tf_op jit(solution)/shard_map/ppermute | solution.py:214
  3.2 1.7 %own_state.1 = (f32[2,32,128]{2,1,0:T(8,128)S(1)}, f32[256,128]{1,0:T(8,128)S(1)}, f32[64,128]{1,0:T(8,128)S(1)}, f32[64,128]{1,0:T(8,128)S(1)}, f32[2,16,32,128...) custom-call(f32[256,128]{1,0:T(8,128)} %x_hbm.1, f32[64,128]{1,0:T(8,128)} %bitcast.332, ...), custom_call_target="tpu_custom_call" | custom-call | tf_op jit(solution)/shard_map/own_state/pallas_call | solution.py:215
  4.9 0.0 collective-permute-done.x_ref
  4.9 0.7 %chip_state.1 = (f32[2,32,128]{2,1,0:T(8,128)S(1)}, f32[2,32,128]{2,1,0:T(8,128)S(1)}) custom-call(f32[256,128]{1,0:T(8,128)S(1)} %collective-permute-done.x_ref, f32[2,16,32,128]{3,2,1,0:T(8,128)S(1)} %get-tuple-element.44.table_ref, f32[2,32,128]{2,1,0:T(8,128)S(1)} %get-tuple-element.45.jump_ref, f32[2,32,128]{2,1,0:T(8,128)S(1)} %get-tuple-element.49.block_ref.refs_0_, ...), custom_call_target="tpu_custom_call" | custom-call | tf_op jit(solution)/shard_map/chip_state/pallas_call | solution.py:231
  5.7 1.3 %collective-permute-start.1 = (f32[2,32,128]{2,1,0:T(8,128)S(1)}, f32[2,32,128]{2,1,0:T(8,128)S(1)}, u32[]{:S(2)}, u32[]{:S(2)}) collective-permute-start(f32[2,32,128]{2,1,0:T(8,128)S(1)} %get-tuple-element.48), channel_id=1, source_target_pairs={{0,8},{2,10},{4,12},{6,14},{8,0},{10,2},{12,4},{14,6},{16,24},{18,... | collective-permute-start | bytes 98312 | tf_op jit(solution)/shard_map/ppermute | solution.py:239
  7.0 0.9 %collective-permute-start.2 = (f32[2,32,128]{2,1,0:T(8,128)S(1)}, f32[2,32,128]{2,1,0:T(8,128)S(1)}, u32[]{:S(2)}, u32[]{:S(2)}) collective-permute-start(f32[2,32,128]{2,1,0:T(8,128)S(1)} %get-tuple-element.48), channel_id=1, source_target_pairs={{0,14},{2,12},{4,10},{6,8},{8,6},{10,4},{12,2},{14,0},{16,30},{18,... | collective-permute-start | bytes 98312 | tf_op jit(solution)/shard_map/ppermute | solution.py:239
  7.9 0.8 %collective-permute-start.3 = (f32[2,32,128]{2,1,0:T(8,128)S(1)}, f32[2,32,128]{2,1,0:T(8,128)S(1)}, u32[]{:S(2)}, u32[]{:S(2)}) collective-permute-start(f32[2,32,128]{2,1,0:T(8,128)S(1)} %get-tuple-element.48), channel_id=1, source_target_pairs={{0,6},{2,4},{4,2},{6,0},{8,14},{10,12},{12,10},{14,8},{16,22},{18,... | collective-permute-start | bytes 98312 | tf_op jit(solution)/shard_map/ppermute | solution.py:239
  8.7 0.1 chip_powers.1
  8.8 1.1 %tables.1 = (f32[2,64,128]{2,1,0:T(8,128)S(1)}, f32[2,64,128]{2,1,0:T(8,128)S(1)}, f32[2,16,64,128]{3,2,1,0:T(8,128)S(1)}, f32[2,64,128]{2,1,0:T(8,128)S(1)}, f32[1,128]{1,0:T(1,128)S(1)}) custom-call(f32[64,128]{1,0:T(8,128)S(1)} %get-tuple-element.52.refs_1_.decay_ref, f32[64,128]{1,0:T(8,128)S(1)} %get-tuple-element.51.refs_2_.freq_ref, ...), custom_call_target="tpu_custom_call" | custom-call | tf_op jit(solution)/shard_map/tables/pallas_call | solution.py:247
  9.9 0.1 collective-permute-done.1
  10.0 1.5 %collective-permute-done.2 = f32[2,32,128]{2,1,0:T(8,128)S(1)} collective-permute-done((f32[2,32,128]{2,1,0:T(8,128)S(1)}, f32[2,32,128]{2,1,0:T(8,128)S(1)}, u32[]{:S(2)}, u32[]{:S(2)}) %collective-permute-start.2) | collective-permute-done | bytes 32800 | tf_op jit(solution)/shard_map/ppermute | solution.py:239
  11.6 3.1 %collective-permute-start.4 = (f32[2,32,128]{2,1,0:T(8,128)S(1)}, f32[2,32,128]{2,1,0:T(8,128)S(1)}, u32[]{:S(2)}, u32[]{:S(2)}) collective-permute-start(f32[2,32,128]{2,1,0:T(8,128)S(1)} %pad_maximum_fusion), channel_id=1, source_target_pairs={{0,32},{2,34},{4,36},{6,38},{8,40},{10,42},{12,44},{14,46},{16,48}... | collective-permute-start | bytes 98312 | tf_op jit(solution)/shard_map/ppermute | solution.py:239
  14.6 1.6 %collective-permute-start.5 = (f32[2,32,128]{2,1,0:T(8,128)S(1)}, f32[2,32,128]{2,1,0:T(8,128)S(1)}, u32[]{:S(2)}, u32[]{:S(2)}) collective-permute-start(f32[2,32,128]{2,1,0:T(8,128)S(1)} %pad_maximum_fusion), channel_id=1, source_target_pairs={{0,50},{2,48},{4,54},{6,52},{8,58},{10,56},{12,62},{14,60},{16,34}... | collective-permute-start | bytes 98312 | tf_op jit(solution)/shard_map/ppermute | solution.py:239
  16.3 0.5 %collective-permute-start.6 = (f32[2,32,128]{2,1,0:T(8,128)S(1)}, f32[2,32,128]{2,1,0:T(8,128)S(1)}, u32[]{:S(2)}, u32[]{:S(2)}) collective-permute-start(f32[2,32,128]{2,1,0:T(8,128)S(1)} %pad_maximum_fusion), channel_id=1, source_target_pairs={{0,18},{2,16},{4,22},{6,20},{8,26},{10,24},{12,30},{14,28},{16,2},... | collective-permute-start | bytes 98312 | tf_op jit(solution)/shard_map/ppermute | solution.py:239
  16.7 1.4 %taps.1.taps_ref = f32[256,128]{1,0:T(8,128)S(1)} custom-call(f32[2,64,128]{2,1,0:T(8,128)S(1)} %get-tuple-element.59.amp_ref, f32[2,16,64,128]{3,2,1,0:T(8,128)S(1)} %get-tuple-element.60.table_ref, f32[2,64,128]{2,1,0:T(8,128)S(1)} %get-tuple-element.61.jump_ref), custom_call_target="tpu_custom_call" | custom-call | tf_op jit(solution)/shard_map/taps/pallas_call | solution.py:260
  18.1 2.0 %collective-permute-done.5 = f32[2,32,128]{2,1,0:T(8,128)S(1)} collective-permute-done((f32[2,32,128]{2,1,0:T(8,128)S(1)}, f32[2,32,128]{2,1,0:T(8,128)S(1)}, u32[]{:S(2)}, u32[]{:S(2)}) %collective-permute-start.5) | collective-permute-done | bytes 32800 | tf_op jit(solution)/shard_map/ppermute | solution.py:239
  20.2 0.1 collective-permute-done.6
  20.4 2.8 %collective-permute-start.7 = (f32[2,32,128]{2,1,0:T(8,128)S(1)}, f32[2,32,128]{2,1,0:T(8,128)S(1)}, u32[]{:S(2)}, u32[]{:S(2)}) collective-permute-start(f32[2,32,128]{2,1,0:T(8,128)S(1)} %pad_maximum_fusion.1), channel_id=1, source_target_pairs={{0,128},{2,130},{4,132},{6,134},{8,136},{10,138},{12,140},{14,142}... | collective-permute-start | bytes 98312 | tf_op jit(solution)/shard_map/ppermute | solution.py:239
  23.2 1.4 %collective-permute-start.8 = (f32[2,32,128]{2,1,0:T(8,128)S(1)}, f32[2,32,128]{2,1,0:T(8,128)S(1)}, u32[]{:S(2)}, u32[]{:S(2)}) collective-permute-start(f32[2,32,128]{2,1,0:T(8,128)S(1)} %pad_maximum_fusion.1), channel_id=1, source_target_pairs={{0,194},{2,192},{4,198},{6,196},{8,202},{10,200},{12,206},{14,204}... | collective-permute-start | bytes 98312 | tf_op jit(solution)/shard_map/ppermute | solution.py:239
  24.6 0.0 collective-permute-start.9
  24.6 1.9 %local.1.base_ref = f32[256,128]{1,0:T(8,128)S(1)} custom-call(f32[256,128]{1,0:T(8,128)S(1)} %get-tuple-element.66.x_ref, f32[256,128]{1,0:T(8,128)S(1)} %taps.1.taps_ref, f32[1,128]{1,0:T(1,128)} %bitcast.337), custom_call_target="tpu_custom_call" | custom-call | tf_op jit(solution)/shard_map/local/pallas_call | solution.py:265
  26.5 0.0 collective-permute-done.7
  26.5 1.8 %collective-permute-done.8 = f32[2,32,128]{2,1,0:T(8,128)S(1)} collective-permute-done((f32[2,32,128]{2,1,0:T(8,128)S(1)}, f32[2,32,128]{2,1,0:T(8,128)S(1)}, u32[]{:S(2)}, u32[]{:S(2)}) %collective-permute-start.8) | collective-permute-done | bytes 32800 | tf_op jit(solution)/shard_map/ppermute | solution.py:239
  28.3 0.0 collective-permute-done.9
  28.3 0.1 multiply_subtract_fusion
  28.4 0.5 %collective-permute-start.10 = (f32[2,32,128]{2,1,0:T(8,128)S(1)}, f32[2,32,128]{2,1,0:T(8,128)S(1)}, u32[]{:S(2)}, u32[]{:S(2)}) collective-permute-start(f32[2,32,128]{2,1,0:T(8,128)S(1)} %get-tuple-element.95), channel_id=1, source_target_pairs={{0,2},{2,0},{4,6},{6,4},{8,10},{10,8},{12,14},{14,12},{16,18},{18,... | collective-permute-start | bytes 98312 | tf_op jit(solution)/shard_map/ppermute | solution.py:296
  28.9 0.8 %own_half.1.base_ref = f32[256,128]{1,0:T(8,128)S(1)} custom-call(f32[2,32,128]{2,1,0:T(8,128)S(1)} %get-tuple-element.94.carry_ref, f32[2,64,128]{2,1,0:T(8,128)S(1)} %get-tuple-element.72.amp_ref, f32[2,16,64,128]{3,2,1,0:T(8,128)S(1)} %get-tuple-element.60.table_ref, f32[2,64,128]{2,1,0:T(8,128)S(1)} %get-tuple-element.61.jump_ref, ...), custom_call_target="tpu_custom_call" | custom-call | tf_op jit(solution)/shard_map/own_half/pallas_call | solution.py:297
  29.7 0.1 collective-permute-done.10.carry_ref
  29.8 1.1 %other_half.1 = (f32[256,128]{1,0:T(8,128)S(1)}, f32[2,256]{1,0:T(2,128)S(1)}) custom-call(f32[2,32,128]{2,1,0:T(8,128)S(1)} %collective-permute-done.10.carry_ref, f32[2,64,128]{2,1,0:T(8,128)S(1)} %get-tuple-element.72.amp_ref, f32[2,16,64,128]{3,2,1,0:T(8,128)S(1)} %get-tuple-element.60.table_ref, f32[2,64,128]{2,1,0:T(8,128)S(1)} %get-tuple-element.61.jump_ref, ...), custom_call_target="tpu_custom_call" | custom-call | tf_op jit(solution)/shard_map/other_half/pallas_call | solution.py:301
  30.9 4.9 %collective-permute-start.11 = (f32[2,256]{1,0:T(2,128)S(1)}, f32[2,256]{1,0:T(2,128)S(1)}, u32[]{:S(2)}, u32[]{:S(2)}) collective-permute-start(f32[2,256]{1,0:T(2,128)S(1)} %get-tuple-element.77.refs_1_), channel_id=1, source_target_pairs={{0,1},{1,0},{2,3},{3,2},{4,5},{5,4},{6,7},{7,6},{8,9},{9,8},{10,11... | collective-permute-start | bytes 6152 | tf_op jit(solution)/shard_map/ppermute | solution.py:307
  35.8 1.5 %collective-permute-done.11.refs_2_ = f32[2,256]{1,0:T(2,128)S(1)} collective-permute-done((f32[2,256]{1,0:T(2,128)S(1)}, f32[2,256]{1,0:T(2,128)S(1)}, u32[]{:S(2)}, u32[]{:S(2)}) %collective-permute-start.11) | collective-permute-done | bytes 2080 | tf_op jit(solution)/shard_map/ppermute | solution.py:307
  37.2 0.9 %norm.1 = f32[256,128]{1,0:T(8,128)} custom-call(f32[256,128]{1,0:T(8,128)S(1)} %get-tuple-element.76.refs_0_, f32[2,256]{1,0:T(2,128)S(1)} %get-tuple-element.77.refs_1_, f32[2,256]{1,0:T(2,128)S(1)} %collective-permute-done.11.refs_2_, f32[1,128]{1,0:T(1,128)S(1)} %get-tuple-element.78.refs_3_), custom_call_target="tpu_custom_call" | custom-call | tf_op jit(solution)/shard_map/norm/pallas_call | solution.py:308
  (11 shorter events, 0.1 us)
Async XLA Ops:
  0.0 4.9 %collective-permute-start = (f32[256,128]{1,0:T(8,128)}, f32[256,128]{1,0:T(8,128)S(1)}, u32[]{:S(2)}, u32[]{:S(2)}) collective-permute-start(f32[256,128]{1,0:T(8,128)} %x_hbm.1), channel_id=1, source_target_pairs={{0,2},{2,0},{4,6},{6,4},{8,10},{10,8},{12,14},{14,12},{16,18},{18,... | collective-permute-start | bytes 393224 | tf_op jit(solution)/shard_map/ppermute | solution.py:214
  5.7 4.4 %collective-permute-start.1 = (f32[2,32,128]{2,1,0:T(8,128)S(1)}, f32[2,32,128]{2,1,0:T(8,128)S(1)}, u32[]{:S(2)}, u32[]{:S(2)}) collective-permute-start(f32[2,32,128]{2,1,0:T(8,128)S(1)} %get-tuple-element.48), channel_id=1, source_target_pairs={{0,8},{2,10},{4,12},{6,14},{8,0},{10,2},{12,4},{14,6},{16,24},{18,... | collective-permute-start | bytes 98312 | tf_op jit(solution)/shard_map/ppermute | solution.py:239
  7.0 4.6 %collective-permute-start.2 = (f32[2,32,128]{2,1,0:T(8,128)S(1)}, f32[2,32,128]{2,1,0:T(8,128)S(1)}, u32[]{:S(2)}, u32[]{:S(2)}) collective-permute-start(f32[2,32,128]{2,1,0:T(8,128)S(1)} %get-tuple-element.48), channel_id=1, source_target_pairs={{0,14},{2,12},{4,10},{6,8},{8,6},{10,4},{12,2},{14,0},{16,30},{18,... | collective-permute-start | bytes 98312 | tf_op jit(solution)/shard_map/ppermute | solution.py:239
  7.9 3.6 %collective-permute-start.3 = (f32[2,32,128]{2,1,0:T(8,128)S(1)}, f32[2,32,128]{2,1,0:T(8,128)S(1)}, u32[]{:S(2)}, u32[]{:S(2)}) collective-permute-start(f32[2,32,128]{2,1,0:T(8,128)S(1)} %get-tuple-element.48), channel_id=1, source_target_pairs={{0,6},{2,4},{4,2},{6,0},{8,14},{10,12},{12,10},{14,8},{16,22},{18,... | collective-permute-start | bytes 98312 | tf_op jit(solution)/shard_map/ppermute | solution.py:239
  11.6 6.6 %collective-permute-start.4 = (f32[2,32,128]{2,1,0:T(8,128)S(1)}, f32[2,32,128]{2,1,0:T(8,128)S(1)}, u32[]{:S(2)}, u32[]{:S(2)}) collective-permute-start(f32[2,32,128]{2,1,0:T(8,128)S(1)} %pad_maximum_fusion), channel_id=1, source_target_pairs={{0,32},{2,34},{4,36},{6,38},{8,40},{10,42},{12,44},{14,46},{16,48}... | collective-permute-start | bytes 98312 | tf_op jit(solution)/shard_map/ppermute | solution.py:239
  14.6 5.5 %collective-permute-start.5 = (f32[2,32,128]{2,1,0:T(8,128)S(1)}, f32[2,32,128]{2,1,0:T(8,128)S(1)}, u32[]{:S(2)}, u32[]{:S(2)}) collective-permute-start(f32[2,32,128]{2,1,0:T(8,128)S(1)} %pad_maximum_fusion), channel_id=1, source_target_pairs={{0,50},{2,48},{4,54},{6,52},{8,58},{10,56},{12,62},{14,60},{16,34}... | collective-permute-start | bytes 98312 | tf_op jit(solution)/shard_map/ppermute | solution.py:239
  16.3 4.0 %collective-permute-start.6 = (f32[2,32,128]{2,1,0:T(8,128)S(1)}, f32[2,32,128]{2,1,0:T(8,128)S(1)}, u32[]{:S(2)}, u32[]{:S(2)}) collective-permute-start(f32[2,32,128]{2,1,0:T(8,128)S(1)} %pad_maximum_fusion), channel_id=1, source_target_pairs={{0,18},{2,16},{4,22},{6,20},{8,26},{10,24},{12,30},{14,28},{16,2},... | collective-permute-start | bytes 98312 | tf_op jit(solution)/shard_map/ppermute | solution.py:239
  20.4 6.2 %collective-permute-start.7 = (f32[2,32,128]{2,1,0:T(8,128)S(1)}, f32[2,32,128]{2,1,0:T(8,128)S(1)}, u32[]{:S(2)}, u32[]{:S(2)}) collective-permute-start(f32[2,32,128]{2,1,0:T(8,128)S(1)} %pad_maximum_fusion.1), channel_id=1, source_target_pairs={{0,128},{2,130},{4,132},{6,134},{8,136},{10,138},{12,140},{14,142}... | collective-permute-start | bytes 98312 | tf_op jit(solution)/shard_map/ppermute | solution.py:239
  23.2 5.1 %collective-permute-start.8 = (f32[2,32,128]{2,1,0:T(8,128)S(1)}, f32[2,32,128]{2,1,0:T(8,128)S(1)}, u32[]{:S(2)}, u32[]{:S(2)}) collective-permute-start(f32[2,32,128]{2,1,0:T(8,128)S(1)} %pad_maximum_fusion.1), channel_id=1, source_target_pairs={{0,194},{2,192},{4,198},{6,196},{8,202},{10,200},{12,206},{14,204}... | collective-permute-start | bytes 98312 | tf_op jit(solution)/shard_map/ppermute | solution.py:239
  24.6 3.7 %collective-permute-start.9 = (f32[2,32,128]{2,1,0:T(8,128)S(1)}, f32[2,32,128]{2,1,0:T(8,128)S(1)}, u32[]{:S(2)}, u32[]{:S(2)}) collective-permute-start(f32[2,32,128]{2,1,0:T(8,128)S(1)} %pad_maximum_fusion.1), channel_id=1, source_target_pairs={{0,66},{2,64},{4,70},{6,68},{8,74},{10,72},{12,78},{14,76},{16,82}... | collective-permute-start | bytes 98312 | tf_op jit(solution)/shard_map/ppermute | solution.py:239
  28.4 1.3 %collective-permute-start.10 = (f32[2,32,128]{2,1,0:T(8,128)S(1)}, f32[2,32,128]{2,1,0:T(8,128)S(1)}, u32[]{:S(2)}, u32[]{:S(2)}) collective-permute-start(f32[2,32,128]{2,1,0:T(8,128)S(1)} %get-tuple-element.95), channel_id=1, source_target_pairs={{0,2},{2,0},{4,6},{6,4},{8,10},{10,8},{12,14},{14,12},{16,18},{18,... | collective-permute-start | bytes 98312 | tf_op jit(solution)/shard_map/ppermute | solution.py:296
  30.9 6.4 %collective-permute-start.11 = (f32[2,256]{1,0:T(2,128)S(1)}, f32[2,256]{1,0:T(2,128)S(1)}, u32[]{:S(2)}, u32[]{:S(2)}) collective-permute-start(f32[2,256]{1,0:T(2,128)S(1)} %get-tuple-element.77.refs_1_), channel_id=1, source_target_pairs={{0,1},{1,0},{2,3},{3,2},{4,5},{5,4},{6,7},{7,6},{8,9},{9,8},{10,11... | collective-permute-start | bytes 6152 | tf_op jit(solution)/shard_map/ppermute | solution.py:307

commit v4 on v3

--- a/solution.py
+++ b/solution.py
@@ -6,8 +6,7 @@
 from jax.sharding import PartitionSpec as P
 
 RADIX = 16
-PRECISE = lax.Precision.HIGHEST
-LEVELS = ((4, 7, 3), (16, 25, 9), (64, 97, 33))
+LEVELS = ((4, 7, 3), (16, 25, 9), (65, 96, 33))
 
 
 def wave(decay, freq, steps):
@@ -46,7 +45,7 @@
 
 def half_of_modes(modes, other=0):
     half, own = modes // 2, lax.axis_index("seq")
-    mine = (own ^ (own >> 1) ^ (own >> 3) ^ (own >> 5) ^ other) & 1
+    mine = (own ^ (own >> 1) ^ (own >> 3) ^ (own >> 5) ^ (own >> 6) ^ other) & 1
     return pl.ds(pl.multiple_of(mine * half, half), half)
 
 
@@ -63,8 +62,8 @@
     decay, freq = decay_ref[mine, :], freq_ref[mine, :]
     zr, zi = wave(decay, freq, 1)
     jump_ref[0], jump_ref[1] = wave(decay, freq, RADIX)
+    fill_powers(table_ref, zr, zi)
     block_ref[0], block_ref[1] = wave(decay, freq, x_ref.shape[0])
-    fill_powers(table_ref, zr, zi)
     copies[2].wait()
     state_ref[0], state_ref[1] = reduced(x_ref, table_ref, jump_ref)
 
@@ -153,8 +152,14 @@
 
 
 def row_sums(values):
-    ones = jnp.ones((8, values.shape[1]), jnp.float32)
-    return lax.dot_general(ones, values, (((1,), (1,)), ((), ())), precision=PRECISE, preferred_element_type=jnp.float32)
+    ones = jnp.ones((8, values.shape[1]), jnp.bfloat16)
+    total = None
+    for _ in range(3):
+        part = values.astype(jnp.bfloat16)
+        values = values - part.astype(jnp.float32)
+        sums = lax.dot_general(ones, part, (((1,), (1,)), ((), ())), preferred_element_type=jnp.float32)
+        total = sums if total is None else total + sums
+    return total
 
 
 def add_carried(carry_ref, amp_ref, table_ref, jump_ref, base_ref, out_ref, partial, other):

time: 38.3 us -> 38.2 us (level)
  transfers between devices with their start and end apart: 12 -> 12, of which waited for: 7 -> 8; matrix products, arithmetic and copies ran while one was open for 0% -> 0% of each run, Pallas kernels for 19% -> 19%
where the time goes in v4:
time: 38.2 us; the launch traced here: 38 us
  starting transfers between devices  21.3 us (56%)
  Pallas kernels  9.68 us (25%)
  waiting for transfers between devices  6.76 us (18%)
    ppermute x9, starting transfers between devices, on_device(): lax.ppermute(total, 'seq', [(i, i ^ distance) for i in range(shards)])  12.1 us
    ppermute x9, waiting for transfers between devices, on_device(): lax.ppermute(total, 'seq', [(i, i ^ distance) for i in range(shards)])  5.53 us
    ppermute x1, starting transfers between devices, on_device(): other = lax.ppermute(stats, 'ch', [(0, 1), (1, 0)])  5.19 us
    ppermute x1, starting transfers between devices, on_device(): other_x = lax.ppermute(signal, 'seq', core_pairs)  3.2 us
    pallas_call x1, Pallas kernels, on_device(): pl.pallas_call(local_kernel, out_shape=vmem(rows, lanes), scratch_shapes=...  1.93 us
    pallas_call x1, Pallas kernels, on_device(): pl.pallas_call(own_state_kernel, in_specs=[pl.BlockSpec(memory_space=pl.A...  1.73 us
    pallas_call x1, Pallas kernels, on_device(): pl.pallas_call(taps_kernel, out_shape=vmem(rows, lanes), scratch_shapes=[...  1.4 us
    ppermute x1, waiting for transfers between devices, on_device(): other = lax.ppermute(stats, 'ch', [(0, 1), (1, 0)])  1.17 us
  transfers between devices with their start and end apart: 12, of which 8 were waited for; matrix products, arithmetic and copies ran while one was open for 0% of the time, Pallas kernels for 19%

profile of v4, /device:TPU:1, one launch (start us, length us, event | category | flops | bytes accessed | tf_op | source)
XLA Modules:
  0.0 38.0 jit_solution(7942033556908384670)
XLA Ops:
  0.0 3.2 %collective-permute-start = (f32[256,128]{1,0:T(8,128)}, f32[256,128]{1,0:T(8,128)S(1)}, u32[]{:S(2)}, u32[]{:S(2)}) collective-permute-start(f32[256,128]{1,0:T(8,128)} %x_hbm.1), channel_id=1, source_target_pairs={{0,2},{2,0},{4,6},{6,4},{8,10},{10,8},{12,14},{14,12},{16,18},{18,... | collective-permute-start | bytes 393224 | tf_op jit(solution)/shard_map/ppermute | solution.py:219
  3.2 1.7 %own_state.1 = (f32[2,32,128]{2,1,0:T(8,128)S(1)}, f32[256,128]{1,0:T(8,128)S(1)}, f32[64,128]{1,0:T(8,128)S(1)}, f32[64,128]{1,0:T(8,128)S(1)}, f32[2,16,32,128...) custom-call(f32[256,128]{1,0:T(8,128)} %x_hbm.1, f32[64,128]{1,0:T(8,128)} %bitcast.332, ...), custom_call_target="tpu_custom_call" | custom-call | tf_op jit(solution)/shard_map/own_state/pallas_call | solution.py:220
  4.9 0.0 collective-permute-done.x_ref
  5.0 0.7 %chip_state.1 = (f32[2,32,128]{2,1,0:T(8,128)S(1)}, f32[2,32,128]{2,1,0:T(8,128)S(1)}) custom-call(f32[256,128]{1,0:T(8,128)S(1)} %collective-permute-done.x_ref, f32[2,16,32,128]{3,2,1,0:T(8,128)S(1)} %get-tuple-element.44.table_ref, f32[2,32,128]{2,1,0:T(8,128)S(1)} %get-tuple-element.45.jump_ref, f32[2,32,128]{2,1,0:T(8,128)S(1)} %get-tuple-element.49.block_ref.refs_0_, ...), custom_call_target="tpu_custom_call" | custom-call | tf_op jit(solution)/shard_map/chip_state/pallas_call | solution.py:236
  5.7 1.3 %collective-permute-start.1 = (f32[2,32,128]{2,1,0:T(8,128)S(1)}, f32[2,32,128]{2,1,0:T(8,128)S(1)}, u32[]{:S(2)}, u32[]{:S(2)}) collective-permute-start(f32[2,32,128]{2,1,0:T(8,128)S(1)} %get-tuple-element.48), channel_id=1, source_target_pairs={{0,8},{2,10},{4,12},{6,14},{8,0},{10,2},{12,4},{14,6},{16,24},{18,... | collective-permute-start | bytes 98312 | tf_op jit(solution)/shard_map/ppermute | solution.py:244
  7.0 0.9 %collective-permute-start.2 = (f32[2,32,128]{2,1,0:T(8,128)S(1)}, f32[2,32,128]{2,1,0:T(8,128)S(1)}, u32[]{:S(2)}, u32[]{:S(2)}) collective-permute-start(f32[2,32,128]{2,1,0:T(8,128)S(1)} %get-tuple-element.48), channel_id=1, source_target_pairs={{0,14},{2,12},{4,10},{6,8},{8,6},{10,4},{12,2},{14,0},{16,30},{18,... | collective-permute-start | bytes 98312 | tf_op jit(solution)/shard_map/ppermute | solution.py:244
  7.9 0.8 %collective-permute-start.3 = (f32[2,32,128]{2,1,0:T(8,128)S(1)}, f32[2,32,128]{2,1,0:T(8,128)S(1)}, u32[]{:S(2)}, u32[]{:S(2)}) collective-permute-start(f32[2,32,128]{2,1,0:T(8,128)S(1)} %get-tuple-element.48), channel_id=1, source_target_pairs={{0,6},{2,4},{4,2},{6,0},{8,14},{10,12},{12,10},{14,8},{16,22},{18,... | collective-permute-start | bytes 98312 | tf_op jit(solution)/shard_map/ppermute | solution.py:244
  8.7 0.1 chip_powers.1
  8.8 1.1 %tables.1 = (f32[2,64,128]{2,1,0:T(8,128)S(1)}, f32[2,64,128]{2,1,0:T(8,128)S(1)}, f32[2,16,64,128]{3,2,1,0:T(8,128)S(1)}, f32[2,64,128]{2,1,0:T(8,128)S(1)}, f32[1,128]{1,0:T(1,128)S(1)}) custom-call(f32[64,128]{1,0:T(8,128)S(1)} %get-tuple-element.52.refs_1_.decay_ref, f32[64,128]{1,0:T(8,128)S(1)} %get-tuple-element.51.refs_2_.freq_ref, ...), custom_call_target="tpu_custom_call" | custom-call | tf_op jit(solution)/shard_map/tables/pallas_call | solution.py:252
  9.9 0.1 collective-permute-done.1
  10.0 1.5 %collective-permute-done.2 = f32[2,32,128]{2,1,0:T(8,128)S(1)} collective-permute-done((f32[2,32,128]{2,1,0:T(8,128)S(1)}, f32[2,32,128]{2,1,0:T(8,128)S(1)}, u32[]{:S(2)}, u32[]{:S(2)}) %collective-permute-start.2) | collective-permute-done | bytes 32800 | tf_op jit(solution)/shard_map/ppermute | solution.py:244
  11.6 3.1 %collective-permute-start.4 = (f32[2,32,128]{2,1,0:T(8,128)S(1)}, f32[2,32,128]{2,1,0:T(8,128)S(1)}, u32[]{:S(2)}, u32[]{:S(2)}) collective-permute-start(f32[2,32,128]{2,1,0:T(8,128)S(1)} %pad_maximum_fusion), channel_id=1, source_target_pairs={{0,32},{2,34},{4,36},{6,38},{8,40},{10,42},{12,44},{14,46},{16,48}... | collective-permute-start | bytes 98312 | tf_op jit(solution)/shard_map/ppermute | solution.py:244
  14.7 1.6 %collective-permute-start.5 = (f32[2,32,128]{2,1,0:T(8,128)S(1)}, f32[2,32,128]{2,1,0:T(8,128)S(1)}, u32[]{:S(2)}, u32[]{:S(2)}) collective-permute-start(f32[2,32,128]{2,1,0:T(8,128)S(1)} %pad_maximum_fusion), channel_id=1, source_target_pairs={{0,50},{2,48},{4,54},{6,52},{8,58},{10,56},{12,62},{14,60},{16,34}... | collective-permute-start | bytes 98312 | tf_op jit(solution)/shard_map/ppermute | solution.py:244
  16.3 0.5 %collective-permute-start.6 = (f32[2,32,128]{2,1,0:T(8,128)S(1)}, f32[2,32,128]{2,1,0:T(8,128)S(1)}, u32[]{:S(2)}, u32[]{:S(2)}) collective-permute-start(f32[2,32,128]{2,1,0:T(8,128)S(1)} %pad_maximum_fusion), channel_id=1, source_target_pairs={{0,18},{2,16},{4,22},{6,20},{8,26},{10,24},{12,30},{14,28},{16,2},... | collective-permute-start | bytes 98312 | tf_op jit(solution)/shard_map/ppermute | solution.py:244
  16.8 1.4 %taps.1.taps_ref = f32[256,128]{1,0:T(8,128)S(1)} custom-call(f32[2,64,128]{2,1,0:T(8,128)S(1)} %get-tuple-element.59.amp_ref, f32[2,16,64,128]{3,2,1,0:T(8,128)S(1)} %get-tuple-element.60.table_ref, f32[2,64,128]{2,1,0:T(8,128)S(1)} %get-tuple-element.61.jump_ref), custom_call_target="tpu_custom_call" | custom-call | tf_op jit(solution)/shard_map/taps/pallas_call | solution.py:265
  18.2 2.0 %collective-permute-done.5 = f32[2,32,128]{2,1,0:T(8,128)S(1)} collective-permute-done((f32[2,32,128]{2,1,0:T(8,128)S(1)}, f32[2,32,128]{2,1,0:T(8,128)S(1)}, u32[]{:S(2)}, u32[]{:S(2)}) %collective-permute-start.5) | collective-permute-done | bytes 32800 | tf_op jit(solution)/shard_map/ppermute | solution.py:244
  20.2 0.1 collective-permute-done.6
  20.4 3.1 %collective-permute-start.7 = (f32[2,32,128]{2,1,0:T(8,128)S(1)}, f32[2,32,128]{2,1,0:T(8,128)S(1)}, u32[]{:S(2)}, u32[]{:S(2)}) collective-permute-start(f32[2,32,128]{2,1,0:T(8,128)S(1)} %pad_maximum_fusion.1), channel_id=1, source_target_pairs={{0,130},{2,128},{4,134},{6,132},{8,138},{10,136},{12,142},{14,140}... | collective-permute-start | bytes 98312 | tf_op jit(solution)/shard_map/ppermute | solution.py:244
  23.5 0.9 %collective-permute-start.8 = (f32[2,32,128]{2,1,0:T(8,128)S(1)}, f32[2,32,128]{2,1,0:T(8,128)S(1)}, u32[]{:S(2)}, u32[]{:S(2)}) collective-permute-start(f32[2,32,128]{2,1,0:T(8,128)S(1)} %pad_maximum_fusion.1), channel_id=1, source_target_pairs={{0,192},{2,194},{4,196},{6,198},{8,200},{10,202},{12,204},{14,206}... | collective-permute-start | bytes 98312 | tf_op jit(solution)/shard_map/ppermute | solution.py:244
  24.3 0.0 collective-permute-start.9
  24.3 1.9 %local.1.base_ref = f32[256,128]{1,0:T(8,128)S(1)} custom-call(f32[256,128]{1,0:T(8,128)S(1)} %get-tuple-element.66.x_ref, f32[256,128]{1,0:T(8,128)S(1)} %taps.1.taps_ref, f32[1,128]{1,0:T(1,128)} %bitcast.337), custom_call_target="tpu_custom_call" | custom-call | tf_op jit(solution)/shard_map/local/pallas_call | solution.py:270
  26.3 0.0 collective-permute-done.7
  26.3 1.2 %collective-permute-done.8 = f32[2,32,128]{2,1,0:T(8,128)S(1)} collective-permute-done((f32[2,32,128]{2,1,0:T(8,128)S(1)}, f32[2,32,128]{2,1,0:T(8,128)S(1)}, u32[]{:S(2)}, u32[]{:S(2)}) %collective-permute-start.8) | collective-permute-done | bytes 32800 | tf_op jit(solution)/shard_map/ppermute | solution.py:244
  27.4 0.6 %collective-permute-done.9 = f32[2,32,128]{2,1,0:T(8,128)S(1)} collective-permute-done((f32[2,32,128]{2,1,0:T(8,128)S(1)}, f32[2,32,128]{2,1,0:T(8,128)S(1)}, u32[]{:S(2)}, u32[]{:S(2)}) %collective-permute-start.9) | collective-permute-done | bytes 32800 | tf_op jit(solution)/shard_map/ppermute | solution.py:244
  28.1 0.1 multiply_subtract_fusion
  28.2 0.8 %collective-permute-start.10 = (f32[2,32,128]{2,1,0:T(8,128)S(1)}, f32[2,32,128]{2,1,0:T(8,128)S(1)}, u32[]{:S(2)}, u32[]{:S(2)}) collective-permute-start(f32[2,32,128]{2,1,0:T(8,128)S(1)} %get-tuple-element.95), channel_id=1, source_target_pairs={{0,2},{2,0},{4,6},{6,4},{8,10},{10,8},{12,14},{14,12},{16,18},{18,... | collective-permute-start | bytes 98312 | tf_op jit(solution)/shard_map/ppermute | solution.py:301
  29.0 0.8 %own_half.1.base_ref = f32[256,128]{1,0:T(8,128)S(1)} custom-call(f32[2,32,128]{2,1,0:T(8,128)S(1)} %get-tuple-element.94.carry_ref, f32[2,64,128]{2,1,0:T(8,128)S(1)} %get-tuple-element.72.amp_ref, f32[2,16,64,128]{3,2,1,0:T(8,128)S(1)} %get-tuple-element.60.table_ref, f32[2,64,128]{2,1,0:T(8,128)S(1)} %get-tuple-element.61.jump_ref, ...), custom_call_target="tpu_custom_call" | custom-call | tf_op jit(solution)/shard_map/own_half/pallas_call | solution.py:302
  29.8 0.1 collective-permute-done.10.carry_ref
  29.8 1.0 %other_half.1 = (f32[256,128]{1,0:T(8,128)S(1)}, f32[2,256]{1,0:T(2,128)S(1)}) custom-call(f32[2,32,128]{2,1,0:T(8,128)S(1)} %collective-permute-done.10.carry_ref, f32[2,64,128]{2,1,0:T(8,128)S(1)} %get-tuple-element.72.amp_ref, f32[2,16,64,128]{3,2,1,0:T(8,128)S(1)} %get-tuple-element.60.table_ref, f32[2,64,128]{2,1,0:T(8,128)S(1)} %get-tuple-element.61.jump_ref, ...), custom_call_target="tpu_custom_call" | custom-call | tf_op jit(solution)/shard_map/other_half/pallas_call | solution.py:306
  30.8 5.2 %collective-permute-start.11 = (f32[2,256]{1,0:T(2,128)S(1)}, f32[2,256]{1,0:T(2,128)S(1)}, u32[]{:S(2)}, u32[]{:S(2)}) collective-permute-start(f32[2,256]{1,0:T(2,128)S(1)} %get-tuple-element.77.refs_1_), channel_id=1, source_target_pairs={{0,1},{1,0},{2,3},{3,2},{4,5},{5,4},{6,7},{7,6},{8,9},{9,8},{10,11... | collective-permute-start | bytes 6152 | tf_op jit(solution)/shard_map/ppermute | solution.py:312
  36.0 1.2 %collective-permute-done.11.refs_2_ = f32[2,256]{1,0:T(2,128)S(1)} collective-permute-done((f32[2,256]{1,0:T(2,128)S(1)}, f32[2,256]{1,0:T(2,128)S(1)}, u32[]{:S(2)}, u32[]{:S(2)}) %collective-permute-start.11) | collective-permute-done | bytes 2080 | tf_op jit(solution)/shard_map/ppermute | solution.py:312
  37.2 0.9 %norm.1 = f32[256,128]{1,0:T(8,128)} custom-call(f32[256,128]{1,0:T(8,128)S(1)} %get-tuple-element.76.refs_0_, f32[2,256]{1,0:T(2,128)S(1)} %get-tuple-element.77.refs_1_, f32[2,256]{1,0:T(2,128)S(1)} %collective-permute-done.11.refs_2_, f32[1,128]{1,0:T(1,128)S(1)} %get-tuple-element.78.refs_3_), custom_call_target="tpu_custom_call" | custom-call | tf_op jit(solution)/shard_map/norm/pallas_call | solution.py:313
  (11 shorter events, 0.1 us)
Async XLA Ops:
  0.0 4.9 %collective-permute-start = (f32[256,128]{1,0:T(8,128)}, f32[256,128]{1,0:T(8,128)S(1)}, u32[]{:S(2)}, u32[]{:S(2)}) collective-permute-start(f32[256,128]{1,0:T(8,128)} %x_hbm.1), channel_id=1, source_target_pairs={{0,2},{2,0},{4,6},{6,4},{8,10},{10,8},{12,14},{14,12},{16,18},{18,... | collective-permute-start | bytes 393224 | tf_op jit(solution)/shard_map/ppermute | solution.py:219
  5.7 4.4 %collective-permute-start.1 = (f32[2,32,128]{2,1,0:T(8,128)S(1)}, f32[2,32,128]{2,1,0:T(8,128)S(1)}, u32[]{:S(2)}, u32[]{:S(2)}) collective-permute-start(f32[2,32,128]{2,1,0:T(8,128)S(1)} %get-tuple-element.48), channel_id=1, source_target_pairs={{0,8},{2,10},{4,12},{6,14},{8,0},{10,2},{12,4},{14,6},{16,24},{18,... | collective-permute-start | bytes 98312 | tf_op jit(solution)/shard_map/ppermute | solution.py:244
  7.0 4.6 %collective-permute-start.2 = (f32[2,32,128]{2,1,0:T(8,128)S(1)}, f32[2,32,128]{2,1,0:T(8,128)S(1)}, u32[]{:S(2)}, u32[]{:S(2)}) collective-permute-start(f32[2,32,128]{2,1,0:T(8,128)S(1)} %get-tuple-element.48), channel_id=1, source_target_pairs={{0,14},{2,12},{4,10},{6,8},{8,6},{10,4},{12,2},{14,0},{16,30},{18,... | collective-permute-start | bytes 98312 | tf_op jit(solution)/shard_map/ppermute | solution.py:244
  7.9 3.6 %collective-permute-start.3 = (f32[2,32,128]{2,1,0:T(8,128)S(1)}, f32[2,32,128]{2,1,0:T(8,128)S(1)}, u32[]{:S(2)}, u32[]{:S(2)}) collective-permute-start(f32[2,32,128]{2,1,0:T(8,128)S(1)} %get-tuple-element.48), channel_id=1, source_target_pairs={{0,6},{2,4},{4,2},{6,0},{8,14},{10,12},{12,10},{14,8},{16,22},{18,... | collective-permute-start | bytes 98312 | tf_op jit(solution)/shard_map/ppermute | solution.py:244
  11.6 6.6 %collective-permute-start.4 = (f32[2,32,128]{2,1,0:T(8,128)S(1)}, f32[2,32,128]{2,1,0:T(8,128)S(1)}, u32[]{:S(2)}, u32[]{:S(2)}) collective-permute-start(f32[2,32,128]{2,1,0:T(8,128)S(1)} %pad_maximum_fusion), channel_id=1, source_target_pairs={{0,32},{2,34},{4,36},{6,38},{8,40},{10,42},{12,44},{14,46},{16,48}... | collective-permute-start | bytes 98312 | tf_op jit(solution)/shard_map/ppermute | solution.py:244
  14.7 5.5 %collective-permute-start.5 = (f32[2,32,128]{2,1,0:T(8,128)S(1)}, f32[2,32,128]{2,1,0:T(8,128)S(1)}, u32[]{:S(2)}, u32[]{:S(2)}) collective-permute-start(f32[2,32,128]{2,1,0:T(8,128)S(1)} %pad_maximum_fusion), channel_id=1, source_target_pairs={{0,50},{2,48},{4,54},{6,52},{8,58},{10,56},{12,62},{14,60},{16,34}... | collective-permute-start | bytes 98312 | tf_op jit(solution)/shard_map/ppermute | solution.py:244
  16.3 4.0 %collective-permute-start.6 = (f32[2,32,128]{2,1,0:T(8,128)S(1)}, f32[2,32,128]{2,1,0:T(8,128)S(1)}, u32[]{:S(2)}, u32[]{:S(2)}) collective-permute-start(f32[2,32,128]{2,1,0:T(8,128)S(1)} %pad_maximum_fusion), channel_id=1, source_target_pairs={{0,18},{2,16},{4,22},{6,20},{8,26},{10,24},{12,30},{14,28},{16,2},... | collective-permute-start | bytes 98312 | tf_op jit(solution)/shard_map/ppermute | solution.py:244
  20.4 5.9 %collective-permute-start.7 = (f32[2,32,128]{2,1,0:T(8,128)S(1)}, f32[2,32,128]{2,1,0:T(8,128)S(1)}, u32[]{:S(2)}, u32[]{:S(2)}) collective-permute-start(f32[2,32,128]{2,1,0:T(8,128)S(1)} %pad_maximum_fusion.1), channel_id=1, source_target_pairs={{0,130},{2,128},{4,134},{6,132},{8,138},{10,136},{12,142},{14,140}... | collective-permute-start | bytes 98312 | tf_op jit(solution)/shard_map/ppermute | solution.py:244
  23.5 4.0 %collective-permute-start.8 = (f32[2,32,128]{2,1,0:T(8,128)S(1)}, f32[2,32,128]{2,1,0:T(8,128)S(1)}, u32[]{:S(2)}, u32[]{:S(2)}) collective-permute-start(f32[2,32,128]{2,1,0:T(8,128)S(1)} %pad_maximum_fusion.1), channel_id=1, source_target_pairs={{0,192},{2,194},{4,196},{6,198},{8,200},{10,202},{12,204},{14,206}... | collective-permute-start | bytes 98312 | tf_op jit(solution)/shard_map/ppermute | solution.py:244
  24.3 3.7 %collective-permute-start.9 = (f32[2,32,128]{2,1,0:T(8,128)S(1)}, f32[2,32,128]{2,1,0:T(8,128)S(1)}, u32[]{:S(2)}, u32[]{:S(2)}) collective-permute-start(f32[2,32,128]{2,1,0:T(8,128)S(1)} %pad_maximum_fusion.1), channel_id=1, source_target_pairs={{0,66},{2,64},{4,70},{6,68},{8,74},{10,72},{12,78},{14,76},{16,82}... | collective-permute-start | bytes 98312 | tf_op jit(solution)/shard_map/ppermute | solution.py:244
  28.2 1.6 %collective-permute-start.10 = (f32[2,32,128]{2,1,0:T(8,128)S(1)}, f32[2,32,128]{2,1,0:T(8,128)S(1)}, u32[]{:S(2)}, u32[]{:S(2)}) collective-permute-start(f32[2,32,128]{2,1,0:T(8,128)S(1)} %get-tuple-element.95), channel_id=1, source_target_pairs={{0,2},{2,0},{4,6},{6,4},{8,10},{10,8},{12,14},{14,12},{16,18},{18,... | collective-permute-start | bytes 98312 | tf_op jit(solution)/shard_map/ppermute | solution.py:301
  30.8 6.4 %collective-permute-start.11 = (f32[2,256]{1,0:T(2,128)S(1)}, f32[2,256]{1,0:T(2,128)S(1)}, u32[]{:S(2)}, u32[]{:S(2)}) collective-permute-start(f32[2,256]{1,0:T(2,128)S(1)} %get-tuple-element.77.refs_1_), channel_id=1, source_target_pairs={{0,1},{1,0},{2,3},{3,2},{4,5},{5,4},{6,7},{7,6},{8,9},{9,8},{10,11... | collective-permute-start | bytes 6152 | tf_op jit(solution)/shard_map/ppermute | solution.py:312
